TPU v7x, 32 devices: a whole 2x2x4 slice. The times are simulated.
32 devices in a mesh: group: 8 (over y, x, core), resp: 4 (over z).
Axes of the slice: x: 2, y: 2, z: 4, core: 2. Of those that a mesh axis runs over, the one named last changes fastest.
Arguments:
- prompt_hidden: bfloat16 [8, 32, 4096], P('group', 'resp'), may hold values from -6 to 6
- kv_weight: bfloat16 [2048, 4096], P('resp'), may hold values from -0.09375 to 0.09375
- queries: bfloat16 [8, 512, 4096], P('group', 'resp'), may hold values from -150 to 150
- resp_keys: bfloat16 [8, 512, 1024], P('group', 'resp'), may hold values from -5 to 5
- resp_values: bfloat16 [8, 512, 1024], P('group', 'resp'), may hold values from -6 to 6
- upstream: bfloat16 [8, 512, 4096], P('group', 'resp'), may hold values from -6 to 6
- signs: int32 [8, 512], P('group', 'resp'), may hold values from -1 to 1
- lengths: int32 [8, 4], P('group', 'resp'), may hold values from 64 to 128
Outputs:
- grad_keys: bfloat16 [8, 512, 1024], P('group', 'resp')
- grad_values: bfloat16 [8, 512, 1024], P('group', 'resp')
- grad_weight: float32 [2048, 4096], P('resp', 'group')
All inputs are finite; a program needn't handle non-finite values.
Results may differ from a plain program's by a relative error of at most 0.025.
Values may be sent and summed in bfloat16 or wider, within the bound.
No kernel may reach another device: no remote copies, remote signals or barrier semaphores. Data moves between devices by JAX's collectives and lax.ppermute only.
A program may use at most 64 MiB of HBM per device.

v0:
```python
import functools
import math

import jax
import jax.numpy as jnp
from jax import lax
from jax.experimental import pallas as pl
from jax.experimental.pallas import tpu as pltpu
from jax.sharding import PartitionSpec as P


HEADS = 32
KV_HEADS = 8
HEAD = 128
PER_HEAD = HEADS // KV_HEADS
SCALING = 1.0 / math.sqrt(HEAD)
LOG2_SCALE = SCALING * math.log2(math.e)


def dot(left, right, left_dim, right_dim):
    return lax.dot_general(
        left, right, (((left_dim,), (right_dim,)), ((), ())), preferred_element_type=jnp.float32
    )


def partner_of(index, step, count):
    if count & (count - 1) == 0:
        return index ^ step
    return (index + step) % count


def sender_to(index, step, count):
    if count & (count - 1) == 0:
        return index ^ step
    return lax.rem(index - step + count, count)


def stacked(ref, start):
    return jnp.concatenate(
        [ref[0, :, pl.ds(start + i * HEAD, HEAD)] for i in range(PER_HEAD)], axis=0
    )


def mask_kernel(mask_ref):
    later = lax.broadcasted_iota(jnp.int32, mask_ref.shape, 0) > lax.broadcasted_iota(
        jnp.int32, mask_ref.shape, 1
    )
    mask_ref[...] = jnp.where(later, -jnp.inf, 0.0)


def own_kernel(
    mask_ref, q_ref, u_ref, k_ref, v_ref, signs_ref, lengths_ref, exp_ref, dots_ref, stats_ref
):
    seq = q_ref.shape[1]
    live = lax.broadcasted_iota(jnp.int32, signs_ref.shape, 1) < lengths_ref[...]
    row_weights = jnp.where(live, signs_ref[...], 0).astype(jnp.float32)
    for j in range(KV_HEADS):
        keys = k_ref[0, :, j * HEAD : (j + 1) * HEAD]
        values = v_ref[0, :, j * HEAD : (j + 1) * HEAD]
        for h in range(j * PER_HEAD, (j + 1) * PER_HEAD):
            cols = slice(h * HEAD, (h + 1) * HEAD)
            at = slice(h * seq, (h + 1) * seq)
            scores = dot(keys, q_ref[0, :, cols], 1, 1) + mask_ref[...]
            highest = jnp.max(scores, axis=0, keepdims=True)
            weight = jnp.exp2((scores - highest) * LOG2_SCALE)
            dots = dot(values, u_ref[0, :, cols], 1, 1)
            exp_ref[:, at] = weight
            dots_ref[:, at] = dots
            stats_ref[0:1, at] = highest
            stats_ref[1:2, at] = jnp.sum(weight, axis=0, keepdims=True)
            stats_ref[2:3, at] = jnp.sum(weight * dots, axis=0, keepdims=True)
            stats_ref[3:4, at] = row_weights


def project_kernel(count, *refs):
    blocks, w_ref = refs[:count], refs[count]
    kv_ref, hidden_ref = refs[count + 1 :]
    me = lax.axis_index("resp")
    for step in range(count):
        hidden_ref[sender_to(me, step, count)] = blocks[step][0]
    hidden = hidden_ref[...].reshape(-1, hidden_ref.shape[-1])
    kv_ref[...] = dot(hidden, w_ref[...], 1, 1).astype(jnp.bfloat16)


def spread_kernel(chips, mine_ref, partner_ref, *outs):
    me = lax.axis_index("group")
    chip, core = me // 2, lax.rem(me, 2)
    width = outs[0].shape[-1]
    for step in range(chips):
        group = 2 * partner_of(chip, step, chips) + core
        at = pl.ds(pl.multiple_of(group * width, width), width)
        for side, ref in enumerate((mine_ref, partner_ref)):
            outs[step][side] = ref[:, :, at].reshape(outs[step].shape[1:])


def prompt_head(at, queries, upstream, keys, values, stats_ref):
    scores = dot(keys, queries, 1, 1)
    dots = dot(values, upstream, 1, 1)
    own_highest = stats_ref[0:1, at]
    highest = jnp.maximum(own_highest, jnp.max(scores, axis=0, keepdims=True))
    own_factor = jnp.exp2((own_highest - highest) * LOG2_SCALE)
    weight = jnp.exp2((scores - highest) * LOG2_SCALE)
    total = stats_ref[1:2, at] * own_factor + jnp.sum(weight, axis=0, keepdims=True)
    mixed = stats_ref[2:3, at] * own_factor + jnp.sum(weight * dots, axis=0, keepdims=True)
    inverse = 1.0 / total
    delta = mixed * inverse
    factor = stats_ref[3:4, at] * inverse
    probs = weight * factor
    grads = probs * (dots - delta)
    key_terms = dot(grads.astype(jnp.bfloat16), queries, 1, 0) * SCALING
    value_terms = dot(probs.astype(jnp.bfloat16), upstream, 1, 0)
    return key_terms, value_terms, own_factor * factor, delta


def pair_kernel(
    count, step, q_ref, u_ref, stats_ref, near_ref, far_ref,
    scale_ref, near_terms_ref, far_terms_ref, kv_ref, terms_ref,
):
    seq = q_ref.shape[1]
    heads = near_ref.shape[1] // HEAD
    index = lax.axis_index("resp") ^ step
    pair, side = lax.rem(index, count // 2), index // (count // 2)
    kv_ref[side] = near_ref[...]
    kv_ref[1 - side] = far_ref[...]
    size = PER_HEAD * HEAD
    for i in range(heads):
        start = pl.multiple_of((pair * heads + i) * size, size)
        queries, upstream = stacked(q_ref, start), stacked(u_ref, start)
        at = slice(i * HEAD, (i + 1) * HEAD)
        stats_at = pl.ds(pl.multiple_of((pair * heads + i) * PER_HEAD * seq, PER_HEAD * seq), PER_HEAD * seq)
        key_terms, value_terms, factor, delta = prompt_head(
            stats_at, queries, upstream, kv_ref[0, :, at], kv_ref[1, :, at], stats_ref
        )
        here = slice(i * PER_HEAD * seq, (i + 1) * PER_HEAD * seq)
        scale_ref[0:1, here] = factor
        scale_ref[1:2, here] = delta
        terms_ref[0, :, at] = key_terms.astype(jnp.bfloat16)
        terms_ref[1, :, at] = value_terms.astype(jnp.bfloat16)
    near_terms_ref[...] = terms_ref[side]
    far_terms_ref[...] = terms_ref[1 - side]


def prompt_kernel(count, q_ref, u_ref, stats_ref, *refs):
    blocks = refs[:count]
    scale_ref = refs[count]
    terms_refs = refs[count + 1 : 2 * count + 1]
    kv_ref, terms_ref = refs[2 * count + 1 :]
    me = lax.axis_index("resp")
    seq = q_ref.shape[1]
    features = blocks[0].shape[1]
    for step in range(count):
        kv_ref[sender_to(me, step, count)] = blocks[step][...]

    def prompt_of(first):
        if features >= HEAD:
            at = first % features
            return kv_ref[first // features, :, at : at + HEAD]
        return jnp.concatenate(
            [kv_ref[(first + i) // features] for i in range(0, HEAD, features)], axis=1
        )

    def put(first, value):
        if features >= HEAD:
            at = first % features
            terms_ref[first // features, :, at : at + HEAD] = value
        else:
            for i in range(0, HEAD, features):
                terms_ref[(first + i) // features] = value[:, i : i + features]

    for j in range(KV_HEADS):
        at = slice(j * PER_HEAD * seq, (j + 1) * PER_HEAD * seq)
        start = j * PER_HEAD * HEAD
        key_terms, value_terms, factor, delta = prompt_head(
            at, stacked(q_ref, start), stacked(u_ref, start),
            prompt_of(j * HEAD), prompt_of((KV_HEADS + j) * HEAD), stats_ref,
        )
        scale_ref[0:1, at] = factor
        scale_ref[1:2, at] = delta
        put(j * HEAD, key_terms)
        put((KV_HEADS + j) * HEAD, value_terms)
    for step in range(count):
        terms_refs[step][...] = terms_ref[partner_of(me, step, count)].astype(jnp.bfloat16)


def own_grad_kernel(steps, count, q_ref, u_ref, exp_ref, dots_ref, *refs):
    seq = q_ref.shape[1]
    gk_ref, gv_ref = refs[len(steps) :]
    for step, scale_ref in zip(steps, refs):
        heads = scale_ref.shape[1] // (PER_HEAD * seq)
        first = 0
        if len(steps) > 1:
            first = lax.rem(lax.axis_index("resp") ^ step, count // 2) * heads
        for j in range(heads):
            probs, grads = [], []
            for h in range(PER_HEAD):
                here = slice((j * PER_HEAD + h) * seq, (j * PER_HEAD + h + 1) * seq)
                start = ((first + j) * PER_HEAD + h) * seq
                at = pl.ds(start if len(steps) == 1 else pl.multiple_of(start, seq), seq)
                prob = exp_ref[:, at] * scale_ref[0:1, here]
                grad = prob * (dots_ref[:, at] - scale_ref[1:2, here])
                probs.append(prob.astype(jnp.bfloat16))
                grads.append(grad.astype(jnp.bfloat16))
            start, column = (first + j) * PER_HEAD * HEAD, (first + j) * HEAD
            if len(steps) > 1:
                start, column = pl.multiple_of(start, HEAD), pl.multiple_of(column, HEAD)
            cols = pl.ds(column, HEAD)
            keys = dot(jnp.concatenate(grads, axis=1), stacked(q_ref, start), 1, 0) * SCALING
            values = dot(jnp.concatenate(probs, axis=1), stacked(u_ref, start), 1, 0)
            gk_ref[0, :, cols] = keys.astype(jnp.bfloat16)
            gv_ref[0, :, cols] = values.astype(jnp.bfloat16)


def sum_kernel(*refs):
    total = refs[0][...].astype(jnp.float32)
    for ref in refs[1:-1]:
        total = total + ref[...].astype(jnp.float32)
    refs[-1][...] = total.astype(jnp.bfloat16)


def weight_kernel(chips, *refs):
    grads, columns, out_ref = refs[: 2 * chips], refs[2 * chips : 3 * chips], refs[3 * chips]
    left = jnp.concatenate([ref[...] for ref in grads], axis=0)
    right = jnp.concatenate([ref[side] for side in range(2) for ref in columns], axis=0)
    out_ref[...] = dot(left, right, 0, 0)


def call(kernel, outs, inputs, scratch=(), kinds={}, flops=0, limit=24):
    size = sum(x.size * x.dtype.itemsize for x in list(inputs) + list(outs))
    return pl.pallas_call(
        kernel,
        out_shape=tuple(outs),
        in_specs=[pl.BlockSpec(memory_space=kinds.get(i, pltpu.VMEM)) for i in range(len(inputs))],
        out_specs=tuple(pl.BlockSpec(memory_space=pltpu.VMEM) for _ in outs),
        scratch_shapes=list(scratch),
        cost_estimate=pl.CostEstimate(flops=flops, bytes_accessed=size, transcendentals=0),
        compiler_params=pltpu.CompilerParams(vmem_limit_bytes=limit << 20),
    )(*inputs)


def shape(dims, dtype):
    return jax.ShapeDtypeStruct(tuple(dims), dtype)


def per_device(
    resps, groups, prompt_hidden, kv_weight, queries, resp_keys, resp_values, upstream, signs, lengths
):
    chips = groups // 2

    def over_resp(value, step):
        pairs = [(i, partner_of(i, step, resps)) for i in range(resps)]
        return lax.ppermute(value, "resp", pairs)

    def over_chips(value, step):
        pairs = [(i, 2 * partner_of(i // 2, step, chips) + i % 2) for i in range(groups)]
        return lax.ppermute(value, "group", pairs)

    def swap(value):
        return lax.ppermute(value, "group", [(i, i ^ 1) for i in range(groups)])

    seq = queries.shape[1]
    rows, width = prompt_hidden.shape[1:]
    features = kv_weight.shape[0]
    prompt = rows * resps
    unit = 2 * seq * seq * HEAD * HEADS
    bf16, f32 = jnp.bfloat16, jnp.float32
    block = shape((prompt, features), bf16)

    (mask,) = call(mask_kernel, [shape((seq, seq), f32)], [], flops=MASK_FLOPS)
    hidden_blocks = [prompt_hidden] + [over_resp(prompt_hidden, s) for s in range(1, resps)]
    wide = shape((seq, HEADS * seq), f32)
    exps, dots, stats = call(
        own_kernel,
        [wide, wide, shape((8, HEADS * seq), f32)],
        [mask, queries, upstream, resp_keys, resp_values, signs, lengths],
        flops=OWN_FLOPS,
    )
    prompt_kv, hidden = call(
        functools.partial(project_kernel, resps),
        [block, shape((resps, rows, width), bf16)],
        hidden_blocks + [kv_weight],
        flops=2 * prompt * features * width,
    )
    kv_blocks = [prompt_kv] + [over_resp(prompt_kv, s) for s in range(1, resps)]
    terms = [None] * resps
    if paired(resps, features):
        half = resps // 2
        steps, scales = tuple(range(half)), []
        for s in steps:
            scale, terms[s], terms[s + half] = call(
                functools.partial(pair_kernel, resps, s),
                [shape((8, features // HEAD * PER_HEAD * seq), f32), block, block],
                [queries, upstream, stats, kv_blocks[s], kv_blocks[s + half]],
                scratch=[pltpu.VMEM((2, prompt, features), bf16)] * 2,
                flops=unit // half,
            )
            scales.append(scale)
    else:
        steps = (0,)
        scale, *terms = call(
            functools.partial(prompt_kernel, resps),
            [shape((8, HEADS * seq), f32)] + [block] * resps,
            [queries, upstream, stats] + kv_blocks,
            scratch=[
                pltpu.VMEM((resps, prompt, features), bf16),
                pltpu.VMEM((resps, prompt, features), f32),
            ],
            flops=unit,
        )
        scales = [scale]
    terms = [terms[0]] + [over_resp(terms[s], s) for s in range(1, resps)]
    columns = width // groups
    spread = call(
        functools.partial(spread_kernel, chips),
        [shape((2, prompt, columns), bf16)] * chips,
        [hidden, swap(hidden)],
    )
    hidden_columns = [spread[0]] + [over_chips(spread[s], s) for s in range(1, chips)]
    (prompt_grad,) = call(sum_kernel, [block], terms)
    grad_columns = [prompt_grad] + [over_chips(prompt_grad, s) for s in range(1, chips)]
    grad_columns = grad_columns + [swap(x) for x in grad_columns]
    grad_keys, grad_values = call(
        functools.partial(own_grad_kernel, steps, resps),
        [shape(resp_keys.shape, bf16), shape(resp_values.shape, bf16)],
        [queries, upstream, exps, dots] + scales,
        flops=2 * unit,
    )
    (grad_weight,) = call(
        functools.partial(weight_kernel, chips),
        [shape((features, columns), f32)],
        grad_columns + hidden_columns,
        flops=2 * groups * prompt * features * columns,
    )
    return (grad_keys, grad_values, grad_weight)


def paired(resps, features):
    return resps > 1 and resps & (resps - 1) == 0 and features % HEAD == 0


MASK_FLOPS = OWN_FLOPS = 20_000_000_000


def solution(mesh):
    placed = (
        P("group", "resp", None),
        P("resp", None),
        P("group", "resp", None),
        P("group", "resp", None),
        P("group", "resp", None),
        P("group", "resp", None),
        P("group", "resp"),
        P("group", "resp"),
    )

    def body(*args):
        return per_device(mesh.shape["resp"], mesh.shape["group"], *args)

    return jax.shard_map(
        body,
        mesh=mesh,
        in_specs=placed,
        out_specs=(P("group", "resp", None), P("group", "resp", None), P("resp", "group")),
        check_vma=False,
    )
```

profile of v0, /device:TPU:0, one launch (start us, length us, event | category | flops | bytes accessed | tf_op | source)
XLA Modules:
  0.0 44.2 jit_solution(3791649826586014548)
XLA Ops:
  0.6 4.1 %collective-permute-start.1 = (bf16[1,8,4096]{2,1,0:T(8,128)(2,1)}, bf16[1,8,4096]{2,1,0:T(8,128)(2,1)S(1)}, u32[]{:S(2)}, u32[]{:S(2)}) collective-permute-start(bf16[1,8,4096]{2,1,0:T(8,128)(2,1)} %refs_0_.1), channel_id=1, source_target_pairs={{0,2},{1,3},{2,0},{3,1},{4,6},{5,7},{6,4},{7,5},{8,10},{9,11},{10,... | collective-permute-start | bytes 196616 | tf_op jit(solution)/shard_map/ppermute | solution.py:251
  4.8 1.6 %collective-permute-start = (bf16[1,8,4096]{2,1,0:T(8,128)(2,1)}, bf16[1,8,4096]{2,1,0:T(8,128)(2,1)S(1)}, u32[]{:S(2)}, u32[]{:S(2)}) collective-permute-start(bf16[1,8,4096]{2,1,0:T(8,128)(2,1)} %refs_0_.1), channel_id=1, source_target_pairs={{0,1},{1,0},{2,3},{3,2},{4,5},{5,4},{6,7},{7,6},{8,9},{9,8},{10,11... | collective-permute-start | bytes 196616 | tf_op jit(solution)/shard_map/ppermute | solution.py:251
  6.3 0.0 collective-permute-start.2
  7.2 0.0 copy-start
  7.2 0.0 copy-start.1
  7.2 0.0 copy-start.4
  7.2 0.0 copy-start.5
  7.2 0.0 copy-start.6
  7.2 0.8 %collective-permute-done.1.refs_2_ = bf16[1,8,4096]{2,1,0:T(8,128)(2,1)S(1)} collective-permute-done((bf16[1,8,4096]{2,1,0:T(8,128)(2,1)}, bf16[1,8,4096]{2,1,0:T(8,128)(2,1)S(1)}, u32[]{:S(2)}, u32[]{:S(2)}) %collective-permute-start.1) | collective-permute-done | bytes 65568 | tf_op jit(solution)/shard_map/ppermute | solution.py:251
  8.0 1.2 %collective-permute-done.refs_1_ = bf16[1,8,4096]{2,1,0:T(8,128)(2,1)S(1)} collective-permute-done((bf16[1,8,4096]{2,1,0:T(8,128)(2,1)}, bf16[1,8,4096]{2,1,0:T(8,128)(2,1)S(1)}, u32[]{:S(2)}, u32[]{:S(2)}) %collective-permute-start) | collective-permute-done | bytes 65568 | tf_op jit(solution)/shard_map/ppermute | solution.py:251
  9.2 3.4 %collective-permute-done.2.refs_3_ = bf16[1,8,4096]{2,1,0:T(8,128)(2,1)S(1)} collective-permute-done((bf16[1,8,4096]{2,1,0:T(8,128)(2,1)}, bf16[1,8,4096]{2,1,0:T(8,128)(2,1)S(1)}, u32[]{:S(2)}, u32[]{:S(2)}) %collective-permute-start.2) | collective-permute-done | bytes 65568 | tf_op jit(solution)/shard_map/ppermute | solution.py:251
  12.6 1.3 %shard_map.105 = (bf16[32,512]{1,0:T(8,128)(2,1)S(1)}, bf16[4,8,4096]{2,1,0:T(8,128)(2,1)S(1)}) custom-call(bf16[1,8,4096]{2,1,0:T(8,128)(2,1)S(1)} %copy-done.3, bf16[1,8,4096]{2,1,0:T(8,128)(2,1)S(1)} %collective-permute-done.refs_1_, bf16[1,8,4096]{2,1,0:T(8,128)(2,1)S(1)} %collective-permute-done.1.refs_2_, ...), custom_call_target="tpu_custom_call" | custom-call | flops 134217728 | bytes 4751360 | tf_op jit(solution)/shard_map/pallas_call | solution.py:229
  14.0 1.3 %collective-permute-start.5 = (bf16[32,512]{1,0:T(8,128)(2,1)S(1)}, bf16[32,512]{1,0:T(8,128)(2,1)S(1)}, u32[]{:S(2)}, u32[]{:S(2)}) collective-permute-start(bf16[32,512]{1,0:T(8,128)(2,1)S(1)} %get-tuple-element.23.near_ref), channel_id=1, source_target_pairs={{0,3},{1,2},{2,1},{3,0},{4,7},{5,6},{6,5},{7,4},{8,11},{9,10},{10,... | collective-permute-start | bytes 98312 | tf_op jit(solution)/shard_map/ppermute | solution.py:251
  15.2 0.6 %collective-permute-start.4 = (bf16[32,512]{1,0:T(8,128)(2,1)S(1)}, bf16[32,512]{1,0:T(8,128)(2,1)S(1)}, u32[]{:S(2)}, u32[]{:S(2)}) collective-permute-start(bf16[32,512]{1,0:T(8,128)(2,1)S(1)} %get-tuple-element.23.near_ref), channel_id=1, source_target_pairs={{0,1},{1,0},{2,3},{3,2},{4,5},{5,4},{6,7},{7,6},{8,9},{9,8},{10,11... | collective-permute-start | bytes 98312 | tf_op jit(solution)/shard_map/ppermute | solution.py:251
  15.8 2.5 %collective-permute-start.3 = (bf16[32,512]{1,0:T(8,128)(2,1)S(1)}, bf16[32,512]{1,0:T(8,128)(2,1)S(1)}, u32[]{:S(2)}, u32[]{:S(2)}) collective-permute-start(bf16[32,512]{1,0:T(8,128)(2,1)S(1)} %get-tuple-element.23.near_ref), channel_id=1, source_target_pairs={{0,2},{1,3},{2,0},{3,1},{4,6},{5,7},{6,4},{7,5},{8,10},{9,11},{10,... | collective-permute-start | bytes 98312 | tf_op jit(solution)/shard_map/ppermute | solution.py:251
  18.4 0.0 collective-permute-start.16
  18.4 1.7 %shard_map.104 = (f32[128,4096]{1,0:T(8,128)S(1)}, f32[128,4096]{1,0:T(8,128)S(1)}, f32[8,4096]{1,0:T(8,128)S(1)}) custom-call(f32[128,128]{1,0:T(8,128)S(1)} %shard_map.103.mask_ref, bf16[1,128,4096]{2,1,0:T(8,128)(2,1)S(1)} %copy-done, bf16[1,128,4096]{2,1,0:T(8,128)(2,1)S(1)} %copy-done.1, bf16[1,128,1024]{2,1,0:T(8,128)(2,1)S(1)} %copy-done.4, ...), custom_call_target="tpu_custom_call" | custom-call | flops 20000000000 | bytes 7012868 | tf_op jit(solution)/shard_map/pallas_call | solution.py:229
  20.1 0.0 collective-permute-done.5.far_ref
  20.1 0.0 collective-permute-done.4.near_ref
  20.1 1.2 %shard_map.107 = (f32[8,2048]{1,0:T(8,128)S(1)}, bf16[32,512]{1,0:T(8,128)(2,1)S(1)}, bf16[32,512]{1,0:T(8,128)(2,1)S(1)}) custom-call(bf16[1,128,4096]{2,1,0:T(8,128)(2,1)S(1)} %copy-done, bf16[1,128,4096]{2,1,0:T(8,128)(2,1)S(1)} %copy-done.1, f32[8,4096]{1,0:T(8,128)S(1)} %get-tuple-element.22.stats_ref, ...), custom_call_target="tpu_custom_call" | custom-call | flops 67108864 | bytes 2424832 | tf_op jit(solution)/shard_map/pallas_call | solution.py:229
  21.2 0.1 collective-permute-start.6
  21.3 2.0 %collective-permute-start.8 = (bf16[32,512]{1,0:T(8,128)(2,1)S(1)}, bf16[32,512]{1,0:T(8,128)(2,1)S(1)}, u32[]{:S(2)}, u32[]{:S(2)}) collective-permute-start(bf16[32,512]{1,0:T(8,128)(2,1)S(1)} %get-tuple-element.31), channel_id=1, source_target_pairs={{0,3},{1,2},{2,1},{3,0},{4,7},{5,6},{6,5},{7,4},{8,11},{9,10},{10,... | collective-permute-start | bytes 98312 | tf_op jit(solution)/shard_map/ppermute | solution.py:251
  23.3 0.0 collective-permute-done.3.far_ref
  23.3 1.1 %shard_map.106 = (f32[8,2048]{1,0:T(8,128)S(1)}, bf16[32,512]{1,0:T(8,128)(2,1)S(1)}, bf16[32,512]{1,0:T(8,128)(2,1)S(1)}) custom-call(bf16[1,128,4096]{2,1,0:T(8,128)(2,1)S(1)} %copy-done, bf16[1,128,4096]{2,1,0:T(8,128)(2,1)S(1)} %copy-done.1, f32[8,4096]{1,0:T(8,128)S(1)} %get-tuple-element.22.stats_ref, bf16[32,512]{1,0:T(8,128)(2,1)S(1)} %get-tuple-element.23.near_ref, ...), custom_call_target="tpu_custom_call" | custom-call | flops 67108864 | bytes 2424832 | tf_op jit(solution)/shard_map/pallas_call | solution.py:229
  24.4 1.6 %collective-permute-start.7 = (bf16[32,512]{1,0:T(8,128)(2,1)S(1)}, bf16[32,512]{1,0:T(8,128)(2,1)S(1)}, u32[]{:S(2)}, u32[]{:S(2)}) collective-permute-start(bf16[32,512]{1,0:T(8,128)(2,1)S(1)} %get-tuple-element.30), channel_id=1, source_target_pairs={{0,2},{1,3},{2,0},{3,1},{4,6},{5,7},{6,4},{7,5},{8,10},{9,11},{10,... | collective-permute-start | bytes 98312 | tf_op jit(solution)/shard_map/ppermute | solution.py:251
  26.0 1.1 %collective-permute-done.8.refs_3_ = bf16[32,512]{1,0:T(8,128)(2,1)S(1)} collective-permute-done((bf16[32,512]{1,0:T(8,128)(2,1)S(1)}, bf16[32,512]{1,0:T(8,128)(2,1)S(1)}, u32[]{:S(2)}, u32[]{:S(2)}) %collective-permute-start.8) | collective-permute-done | bytes 32800 | tf_op jit(solution)/shard_map/ppermute | solution.py:251
  27.1 2.6 %collective-permute-done.7.refs_2_ = bf16[32,512]{1,0:T(8,128)(2,1)S(1)} collective-permute-done((bf16[32,512]{1,0:T(8,128)(2,1)S(1)}, bf16[32,512]{1,0:T(8,128)(2,1)S(1)}, u32[]{:S(2)}, u32[]{:S(2)}) %collective-permute-start.7) | collective-permute-done | bytes 32800 | tf_op jit(solution)/shard_map/ppermute | solution.py:251
  29.7 2.5 %collective-permute-start.11 = (bf16[32,512]{1,0:T(8,128)(2,1)S(1)}, bf16[32,512]{1,0:T(8,128)(2,1)S(1)}, u32[]{:S(2)}, u32[]{:S(2)}) collective-permute-start(bf16[32,512]{1,0:T(8,128)(2,1)S(1)} %shard_map.109.refs_0_), channel_id=1, source_target_pairs={{0,24},{4,28},{8,16},{12,20},{16,8},{20,12},{24,0},{28,4},{1,25},{... | collective-permute-start | bytes 98312 | tf_op jit(solution)/shard_map/ppermute | solution.py:255
  32.2 0.5 %collective-permute-start.10 = (bf16[32,512]{1,0:T(8,128)(2,1)S(1)}, bf16[32,512]{1,0:T(8,128)(2,1)S(1)}, u32[]{:S(2)}, u32[]{:S(2)}) collective-permute-start(bf16[32,512]{1,0:T(8,128)(2,1)S(1)} %shard_map.109.refs_0_), channel_id=1, source_target_pairs={{0,16},{4,20},{8,24},{12,28},{16,0},{20,4},{24,8},{28,12},{1,17},{... | collective-permute-start | bytes 98312 | tf_op jit(solution)/shard_map/ppermute | solution.py:255
  32.7 0.5 %collective-permute-start.9 = (bf16[32,512]{1,0:T(8,128)(2,1)S(1)}, bf16[32,512]{1,0:T(8,128)(2,1)S(1)}, u32[]{:S(2)}, u32[]{:S(2)}) collective-permute-start(bf16[32,512]{1,0:T(8,128)(2,1)S(1)} %shard_map.109.refs_0_), channel_id=1, source_target_pairs={{0,8},{4,12},{8,0},{12,4},{16,24},{20,28},{24,16},{28,20},{1,9},{5... | collective-permute-start | bytes 98312 | tf_op jit(solution)/shard_map/ppermute | solution.py:255
  33.2 1.3 %collective-permute-done.11.refs_3_ = bf16[32,512]{1,0:T(8,128)(2,1)S(1)} collective-permute-done((bf16[32,512]{1,0:T(8,128)(2,1)S(1)}, bf16[32,512]{1,0:T(8,128)(2,1)S(1)}, u32[]{:S(2)}, u32[]{:S(2)}) %collective-permute-start.11) | collective-permute-done | bytes 32800 | tf_op jit(solution)/shard_map/ppermute | solution.py:255
  34.6 0.0 collective-permute-start.15
  34.6 0.0 collective-permute-done.16.partner_ref
  34.6 1.6 %collective-permute-start.17 = (bf16[2,32,512]{2,1,0:T(8,128)(2,1)S(1)}, bf16[2,32,512]{2,1,0:T(8,128)(2,1)S(1)}, u32[]{:S(2)}, u32[]{:S(2)}) collective-permute-start(bf16[2,32,512]{2,1,0:T(8,128)(2,1)S(1)} %get-tuple-element.34), channel_id=1, source_target_pairs={{0,8},{4,12},{8,0},{12,4},{16,24},{20,28},{24,16},{28,20},{1,9},{5... | collective-permute-start | bytes 196616 | tf_op jit(solution)/shard_map/ppermute | solution.py:255
  36.2 0.0 collective-permute-done.12.refs_4_
  36.2 1.6 %collective-permute-start.18 = (bf16[2,32,512]{2,1,0:T(8,128)(2,1)S(1)}, bf16[2,32,512]{2,1,0:T(8,128)(2,1)S(1)}, u32[]{:S(2)}, u32[]{:S(2)}) collective-permute-start(bf16[2,32,512]{2,1,0:T(8,128)(2,1)S(1)} %get-tuple-element.35), channel_id=1, source_target_pairs={{0,16},{4,20},{8,24},{12,28},{16,0},{20,4},{24,8},{28,12},{1,17},{... | collective-permute-start | bytes 196616 | tf_op jit(solution)/shard_map/ppermute | solution.py:255
  37.7 0.0 collective-permute-done.10.refs_2_
  37.7 0.4 collective-permute-start.19
  38.2 0.0 collective-permute-done.9.refs_1_
  38.2 0.0 collective-permute-start.14
  38.2 0.0 collective-permute-done.15.refs_7_
  38.2 0.5 %collective-permute-start.13 = (bf16[32,512]{1,0:T(8,128)(2,1)S(1)}, bf16[32,512]{1,0:T(8,128)(2,1)S(1)}, u32[]{:S(2)}, u32[]{:S(2)}) collective-permute-start(bf16[32,512]{1,0:T(8,128)(2,1)S(1)} %collective-permute-done.9.refs_1_), channel_id=1, source_target_pairs={{0,4},{4,0},{8,12},{12,8},{16,20},{20,16},{24,28},{28,24},{1,5},{5... | collective-permute-start | bytes 98312 | tf_op jit(solution)/shard_map/ppermute | solution.py:258
  38.7 2.3 %shard_map.108 = (bf16[1,128,1024]{2,1,0:T(8,128)(2,1)}, bf16[1,128,1024]{2,1,0:T(8,128)(2,1)}) custom-call(bf16[1,128,4096]{2,1,0:T(8,128)(2,1)S(1)} %copy-done, bf16[1,128,4096]{2,1,0:T(8,128)(2,1)S(1)} %copy-done.1, f32[128,4096]{1,0:T(8,128)S(1)} %get-tuple-element.20.exp_ref, f32[128,4096]{1,0:T(8,128)S(1)} %get-tuple-element.21.dots_ref, ...), custom_call_target="tpu_custom_call" | custom-call | flops 268435456 | bytes 6946816 | tf_op jit(solution)/shard_map/pallas_call | solution.py:229
  40.9 0.0 collective-permute-done.14.refs_6_
  40.9 0.0 collective-permute-done.13.refs_5_
  40.9 0.0 collective-permute-done.18.refs_10_
  41.0 1.9 %collective-permute-done.19.refs_11_ = bf16[2,32,512]{2,1,0:T(8,128)(2,1)S(1)} collective-permute-done((bf16[2,32,512]{2,1,0:T(8,128)(2,1)S(1)}, bf16[2,32,512]{2,1,0:T(8,128)(2,1)S(1)}, u32[]{:S(2)}, u32[]{:S(2)}) %collective-permute-start.19) | collective-permute-done | bytes 65568 | tf_op jit(solution)/shard_map/ppermute | solution.py:255
  42.9 1.3 %shard_map.111 = f32[512,512]{1,0:T(8,128)} custom-call(bf16[32,512]{1,0:T(8,128)(2,1)S(1)} %shard_map.109.refs_0_, bf16[32,512]{1,0:T(8,128)(2,1)S(1)} %collective-permute-done.9.refs_1_, bf16[32,512]{1,0:T(8,128)(2,1)S(1)} %collective-permute-done.10.refs_2_, bf16[32,512]{1,0:T(8,128)(2,1)S(1)} %collective-permute-done.11.refs_3_, ...), custom_call_target="tpu_custom_call" | custom-call | flops 134217728 | bytes 1572864 | tf_op jit(solution)/shard_map/pallas_call | solution.py:229
  (15 shorter events, 0.1 us)
Async XLA Ops:
  0.6 12.0 %copy-start.3 = (bf16[1,8,4096]{2,1,0:T(8,128)(2,1)S(1)}, bf16[1,8,4096]{2,1,0:T(8,128)(2,1)}, u32[]{:S(2)}) copy-start(bf16[1,8,4096]{2,1,0:T(8,128)(2,1)} %refs_0_.1) | copy-start | bytes 196612
  0.6 7.4 %collective-permute-start.1 = (bf16[1,8,4096]{2,1,0:T(8,128)(2,1)}, bf16[1,8,4096]{2,1,0:T(8,128)(2,1)S(1)}, u32[]{:S(2)}, u32[]{:S(2)}) collective-permute-start(bf16[1,8,4096]{2,1,0:T(8,128)(2,1)} %refs_0_.1), channel_id=1, source_target_pairs={{0,2},{1,3},{2,0},{3,1},{4,6},{5,7},{6,4},{7,5},{8,10},{9,11},{10,... | collective-permute-start | bytes 196616 | tf_op jit(solution)/shard_map/ppermute | solution.py:251
  4.8 4.5 %collective-permute-start = (bf16[1,8,4096]{2,1,0:T(8,128)(2,1)}, bf16[1,8,4096]{2,1,0:T(8,128)(2,1)S(1)}, u32[]{:S(2)}, u32[]{:S(2)}) collective-permute-start(bf16[1,8,4096]{2,1,0:T(8,128)(2,1)} %refs_0_.1), channel_id=1, source_target_pairs={{0,1},{1,0},{2,3},{3,2},{4,5},{5,4},{6,7},{7,6},{8,9},{9,8},{10,11... | collective-permute-start | bytes 196616 | tf_op jit(solution)/shard_map/ppermute | solution.py:251
  6.3 6.3 %collective-permute-start.2 = (bf16[1,8,4096]{2,1,0:T(8,128)(2,1)}, bf16[1,8,4096]{2,1,0:T(8,128)(2,1)S(1)}, u32[]{:S(2)}, u32[]{:S(2)}) collective-permute-start(bf16[1,8,4096]{2,1,0:T(8,128)(2,1)} %refs_0_.1), channel_id=1, source_target_pairs={{0,3},{1,2},{2,1},{3,0},{4,7},{5,6},{6,5},{7,4},{8,11},{9,10},{10,... | collective-permute-start | bytes 196616 | tf_op jit(solution)/shard_map/ppermute | solution.py:251
  6.3 6.3 %copy-start.2 = (bf16[512,4096]{1,0:T(8,128)(2,1)S(1)}, bf16[512,4096]{1,0:T(8,128)(2,1)}, u32[]{:S(2)}) copy-start(bf16[512,4096]{1,0:T(8,128)(2,1)} %refs_4_.1) | copy-start | bytes 12582916
  7.2 11.2 %copy-start = (bf16[1,128,4096]{2,1,0:T(8,128)(2,1)S(1)}, bf16[1,128,4096]{2,1,0:T(8,128)(2,1)}, u32[]{:S(2)}) copy-start(bf16[1,128,4096]{2,1,0:T(8,128)(2,1)} %q_ref.7) | copy-start | bytes 3145732
  7.2 11.2 %copy-start.1 = (bf16[1,128,4096]{2,1,0:T(8,128)(2,1)S(1)}, bf16[1,128,4096]{2,1,0:T(8,128)(2,1)}, u32[]{:S(2)}) copy-start(bf16[1,128,4096]{2,1,0:T(8,128)(2,1)} %u_ref.7) | copy-start | bytes 3145732
  7.2 11.2 %copy-start.4 = (bf16[1,128,1024]{2,1,0:T(8,128)(2,1)S(1)}, bf16[1,128,1024]{2,1,0:T(8,128)(2,1)}, u32[]{:S(2)}) copy-start(bf16[1,128,1024]{2,1,0:T(8,128)(2,1)} %k_ref.1) | copy-start | bytes 786436
  7.2 11.2 %copy-start.5 = (bf16[1,128,1024]{2,1,0:T(8,128)(2,1)S(1)}, bf16[1,128,1024]{2,1,0:T(8,128)(2,1)}, u32[]{:S(2)}) copy-start(bf16[1,128,1024]{2,1,0:T(8,128)(2,1)} %v_ref.1) | copy-start | bytes 786436
  7.2 11.2 %copy-start.6 = (s32[1,128]{1,0:T(1,128)S(1)}, s32[1,128]{1,0:T(1,128)}, u32[]{:S(2)}) copy-start(s32[1,128]{1,0:T(1,128)} %signs_ref.1) | copy-start | bytes 1540
  14.0 6.1 %collective-permute-start.5 = (bf16[32,512]{1,0:T(8,128)(2,1)S(1)}, bf16[32,512]{1,0:T(8,128)(2,1)S(1)}, u32[]{:S(2)}, u32[]{:S(2)}) collective-permute-start(bf16[32,512]{1,0:T(8,128)(2,1)S(1)} %get-tuple-element.23.near_ref), channel_id=1, source_target_pairs={{0,3},{1,2},{2,1},{3,0},{4,7},{5,6},{6,5},{7,4},{8,11},{9,10},{10,... | collective-permute-start | bytes 98312 | tf_op jit(solution)/shard_map/ppermute | solution.py:251
  15.2 4.9 %collective-permute-start.4 = (bf16[32,512]{1,0:T(8,128)(2,1)S(1)}, bf16[32,512]{1,0:T(8,128)(2,1)S(1)}, u32[]{:S(2)}, u32[]{:S(2)}) collective-permute-start(bf16[32,512]{1,0:T(8,128)(2,1)S(1)} %get-tuple-element.23.near_ref), channel_id=1, source_target_pairs={{0,1},{1,0},{2,3},{3,2},{4,5},{5,4},{6,7},{7,6},{8,9},{9,8},{10,11... | collective-permute-start | bytes 98312 | tf_op jit(solution)/shard_map/ppermute | solution.py:251
  15.8 7.4 %collective-permute-start.3 = (bf16[32,512]{1,0:T(8,128)(2,1)S(1)}, bf16[32,512]{1,0:T(8,128)(2,1)S(1)}, u32[]{:S(2)}, u32[]{:S(2)}) collective-permute-start(bf16[32,512]{1,0:T(8,128)(2,1)S(1)} %get-tuple-element.23.near_ref), channel_id=1, source_target_pairs={{0,2},{1,3},{2,0},{3,1},{4,6},{5,7},{6,4},{7,5},{8,10},{9,11},{10,... | collective-permute-start | bytes 98312 | tf_op jit(solution)/shard_map/ppermute | solution.py:251
  18.4 16.2 %collective-permute-start.16 = (bf16[4,8,4096]{2,1,0:T(8,128)(2,1)S(1)}, bf16[4,8,4096]{2,1,0:T(8,128)(2,1)S(1)}, u32[]{:S(2)}, u32[]{:S(2)}) collective-permute-start(bf16[4,8,4096]{2,1,0:T(8,128)(2,1)S(1)} %get-tuple-element.32.mine_ref), channel_id=1, source_target_pairs={{0,4},{4,0},{8,12},{12,8},{16,20},{20,16},{24,28},{28,24},{1,5},{5... | collective-permute-start | bytes 786440 | tf_op jit(solution)/shard_map/ppermute | solution.py:258
  21.2 4.8 %collective-permute-start.6 = (bf16[32,512]{1,0:T(8,128)(2,1)S(1)}, bf16[32,512]{1,0:T(8,128)(2,1)S(1)}, u32[]{:S(2)}, u32[]{:S(2)}) collective-permute-start(bf16[32,512]{1,0:T(8,128)(2,1)S(1)} %get-tuple-element.29), channel_id=1, source_target_pairs={{0,1},{1,0},{2,3},{3,2},{4,5},{5,4},{6,7},{7,6},{8,9},{9,8},{10,11... | collective-permute-start | bytes 98312 | tf_op jit(solution)/shard_map/ppermute | solution.py:251
  21.3 5.8 %collective-permute-start.8 = (bf16[32,512]{1,0:T(8,128)(2,1)S(1)}, bf16[32,512]{1,0:T(8,128)(2,1)S(1)}, u32[]{:S(2)}, u32[]{:S(2)}) collective-permute-start(bf16[32,512]{1,0:T(8,128)(2,1)S(1)} %get-tuple-element.31), channel_id=1, source_target_pairs={{0,3},{1,2},{2,1},{3,0},{4,7},{5,6},{6,5},{7,4},{8,11},{9,10},{10,... | collective-permute-start | bytes 98312 | tf_op jit(solution)/shard_map/ppermute | solution.py:251
  24.4 5.2 %collective-permute-start.7 = (bf16[32,512]{1,0:T(8,128)(2,1)S(1)}, bf16[32,512]{1,0:T(8,128)(2,1)S(1)}, u32[]{:S(2)}, u32[]{:S(2)}) collective-permute-start(bf16[32,512]{1,0:T(8,128)(2,1)S(1)} %get-tuple-element.30), channel_id=1, source_target_pairs={{0,2},{1,3},{2,0},{3,1},{4,6},{5,7},{6,4},{7,5},{8,10},{9,11},{10,... | collective-permute-start | bytes 98312 | tf_op jit(solution)/shard_map/ppermute | solution.py:251
  29.7 4.9 %collective-permute-start.11 = (bf16[32,512]{1,0:T(8,128)(2,1)S(1)}, bf16[32,512]{1,0:T(8,128)(2,1)S(1)}, u32[]{:S(2)}, u32[]{:S(2)}) collective-permute-start(bf16[32,512]{1,0:T(8,128)(2,1)S(1)} %shard_map.109.refs_0_), channel_id=1, source_target_pairs={{0,24},{4,28},{8,16},{12,20},{16,8},{20,12},{24,0},{28,4},{1,25},{... | collective-permute-start | bytes 98312 | tf_op jit(solution)/shard_map/ppermute | solution.py:255
  32.2 4.0 %collective-permute-start.12 = (bf16[32,512]{1,0:T(8,128)(2,1)S(1)}, bf16[32,512]{1,0:T(8,128)(2,1)S(1)}, u32[]{:S(2)}, u32[]{:S(2)}) collective-permute-start(bf16[32,512]{1,0:T(8,128)(2,1)S(1)} %shard_map.109.refs_0_), channel_id=1, source_target_pairs={{0,4},{4,0},{8,12},{12,8},{16,20},{20,16},{24,28},{28,24},{1,5},{5... | collective-permute-start | bytes 98312 | tf_op jit(solution)/shard_map/ppermute | solution.py:258
  32.2 5.5 %collective-permute-start.10 = (bf16[32,512]{1,0:T(8,128)(2,1)S(1)}, bf16[32,512]{1,0:T(8,128)(2,1)S(1)}, u32[]{:S(2)}, u32[]{:S(2)}) collective-permute-start(bf16[32,512]{1,0:T(8,128)(2,1)S(1)} %shard_map.109.refs_0_), channel_id=1, source_target_pairs={{0,16},{4,20},{8,24},{12,28},{16,0},{20,4},{24,8},{28,12},{1,17},{... | collective-permute-start | bytes 98312 | tf_op jit(solution)/shard_map/ppermute | solution.py:255
  32.7 5.5 %collective-permute-start.9 = (bf16[32,512]{1,0:T(8,128)(2,1)S(1)}, bf16[32,512]{1,0:T(8,128)(2,1)S(1)}, u32[]{:S(2)}, u32[]{:S(2)}) collective-permute-start(bf16[32,512]{1,0:T(8,128)(2,1)S(1)} %shard_map.109.refs_0_), channel_id=1, source_target_pairs={{0,8},{4,12},{8,0},{12,4},{16,24},{20,28},{24,16},{28,20},{1,9},{5... | collective-permute-start | bytes 98312 | tf_op jit(solution)/shard_map/ppermute | solution.py:255
  34.6 3.6 %collective-permute-start.15 = (bf16[32,512]{1,0:T(8,128)(2,1)S(1)}, bf16[32,512]{1,0:T(8,128)(2,1)S(1)}, u32[]{:S(2)}, u32[]{:S(2)}) collective-permute-start(bf16[32,512]{1,0:T(8,128)(2,1)S(1)} %collective-permute-done.11.refs_3_), channel_id=1, source_target_pairs={{0,4},{4,0},{8,12},{12,8},{16,20},{20,16},{24,28},{28,24},{1,5},{5... | collective-permute-start | bytes 98312 | tf_op jit(solution)/shard_map/ppermute | solution.py:258
  34.6 6.3 %collective-permute-start.17 = (bf16[2,32,512]{2,1,0:T(8,128)(2,1)S(1)}, bf16[2,32,512]{2,1,0:T(8,128)(2,1)S(1)}, u32[]{:S(2)}, u32[]{:S(2)}) collective-permute-start(bf16[2,32,512]{2,1,0:T(8,128)(2,1)S(1)} %get-tuple-element.34), channel_id=1, source_target_pairs={{0,8},{4,12},{8,0},{12,4},{16,24},{20,28},{24,16},{28,20},{1,9},{5... | collective-permute-start | bytes 196616 | tf_op jit(solution)/shard_map/ppermute | solution.py:255
  36.2 4.8 %collective-permute-start.18 = (bf16[2,32,512]{2,1,0:T(8,128)(2,1)S(1)}, bf16[2,32,512]{2,1,0:T(8,128)(2,1)S(1)}, u32[]{:S(2)}, u32[]{:S(2)}) collective-permute-start(bf16[2,32,512]{2,1,0:T(8,128)(2,1)S(1)} %get-tuple-element.35), channel_id=1, source_target_pairs={{0,16},{4,20},{8,24},{12,28},{16,0},{20,4},{24,8},{28,12},{1,17},{... | collective-permute-start | bytes 196616 | tf_op jit(solution)/shard_map/ppermute | solution.py:255
  37.7 5.2 %collective-permute-start.19 = (bf16[2,32,512]{2,1,0:T(8,128)(2,1)S(1)}, bf16[2,32,512]{2,1,0:T(8,128)(2,1)S(1)}, u32[]{:S(2)}, u32[]{:S(2)}) collective-permute-start(bf16[2,32,512]{2,1,0:T(8,128)(2,1)S(1)} %get-tuple-element.36), channel_id=1, source_target_pairs={{0,24},{4,28},{8,16},{12,20},{16,8},{20,12},{24,0},{28,4},{1,25},{... | collective-permute-start | bytes 196616 | tf_op jit(solution)/shard_map/ppermute | solution.py:255
  38.2 2.8 %collective-permute-start.14 = (bf16[32,512]{1,0:T(8,128)(2,1)S(1)}, bf16[32,512]{1,0:T(8,128)(2,1)S(1)}, u32[]{:S(2)}, u32[]{:S(2)}) collective-permute-start(bf16[32,512]{1,0:T(8,128)(2,1)S(1)} %collective-permute-done.10.refs_2_), channel_id=1, source_target_pairs={{0,4},{4,0},{8,12},{12,8},{16,20},{20,16},{24,28},{28,24},{1,5},{5... | collective-permute-start | bytes 98312 | tf_op jit(solution)/shard_map/ppermute | solution.py:258
  38.2 2.8 %collective-permute-start.13 = (bf16[32,512]{1,0:T(8,128)(2,1)S(1)}, bf16[32,512]{1,0:T(8,128)(2,1)S(1)}, u32[]{:S(2)}, u32[]{:S(2)}) collective-permute-start(bf16[32,512]{1,0:T(8,128)(2,1)S(1)} %collective-permute-done.9.refs_1_), channel_id=1, source_target_pairs={{0,4},{4,0},{8,12},{12,8},{16,20},{20,16},{24,28},{28,24},{1,5},{5... | collective-permute-start | bytes 98312 | tf_op jit(solution)/shard_map/ppermute | solution.py:258
where the time goes:
time: 44.3 us; the launch traced here: 44.2 us
  starting transfers between devices  21.4 us (48%)
  waiting for transfers between devices  12.3 us (28%)
  Pallas kernels  8.87 us (20%)
  between operations  1.59 us (4%)
    ppermute x9, starting transfers between devices, over_resp(): return lax.ppermute(value, 'resp', pairs)  13.7 us
    ppermute x9, waiting for transfers between devices, over_resp(): return lax.ppermute(value, 'resp', pairs)  9.05 us
    pallas_call x9, Pallas kernels, call(): pl.pallas_call(kernel, out_shape=tuple(outs), in_specs=[pl.BlockSpec(memo...  8.87 us
    ppermute x6, starting transfers between devices, over_chips(): return lax.ppermute(value, 'group', pairs)  7.11 us
    ppermute x6, waiting for transfers between devices, over_chips(): return lax.ppermute(value, 'group', pairs)  3.28 us
  transfers between devices with their start and end apart: 20, of which 7 were waited for; matrix products, arithmetic and copies ran while one was open for 0% of the time, Pallas kernels for 14%

commit v1 on v0

--- a/solution.py
+++ b/solution.py
@@ -49,7 +49,8 @@
 
 
 def own_kernel(
-    mask_ref, q_ref, u_ref, k_ref, v_ref, signs_ref, lengths_ref, exp_ref, dots_ref, stats_ref
+    mask_ref, q_ref, u_ref, k_ref, v_ref, signs_ref, lengths_ref,
+    qt_ref, ut_ref, exp_ref, dots_ref, stats_ref,
 ):
     seq = q_ref.shape[1]
     live = lax.broadcasted_iota(jnp.int32, signs_ref.shape, 1) < lengths_ref[...]
@@ -60,16 +61,23 @@
         for h in range(j * PER_HEAD, (j + 1) * PER_HEAD):
             cols = slice(h * HEAD, (h + 1) * HEAD)
             at = slice(h * seq, (h + 1) * seq)
-            scores = dot(keys, q_ref[0, :, cols], 1, 1) + mask_ref[...]
+            queries, upstream = q_ref[0, :, cols].T, u_ref[0, :, cols].T
+            qt_ref[:, at], ut_ref[:, at] = queries, upstream
+            scores = dot(keys, queries, 1, 0) + mask_ref[...]
             highest = jnp.max(scores, axis=0, keepdims=True)
             weight = jnp.exp2((scores - highest) * LOG2_SCALE)
-            dots = dot(values, u_ref[0, :, cols], 1, 1)
+            dots = dot(values, upstream, 1, 0)
             exp_ref[:, at] = weight
             dots_ref[:, at] = dots
             stats_ref[0:1, at] = highest
             stats_ref[1:2, at] = jnp.sum(weight, axis=0, keepdims=True)
             stats_ref[2:3, at] = jnp.sum(weight * dots, axis=0, keepdims=True)
             stats_ref[3:4, at] = row_weights
+
+
+def turn_kernel(w_ref, out_ref):
+    for start in range(0, w_ref.shape[1], HEAD):
+        out_ref[start : start + HEAD] = w_ref[:, start : start + HEAD].T
 
 
 def project_kernel(count, *refs):
@@ -79,7 +87,7 @@
     for step in range(count):
         hidden_ref[sender_to(me, step, count)] = blocks[step][0]
     hidden = hidden_ref[...].reshape(-1, hidden_ref.shape[-1])
-    kv_ref[...] = dot(hidden, w_ref[...], 1, 1).astype(jnp.bfloat16)
+    kv_ref[...] = dot(hidden, w_ref[...], 1, 0).astype(jnp.bfloat16)
 
 
 def spread_kernel(chips, mine_ref, partner_ref, *outs):
@@ -93,9 +101,9 @@
             outs[step][side] = ref[:, :, at].reshape(outs[step].shape[1:])
 
 
-def prompt_head(at, queries, upstream, keys, values, stats_ref):
-    scores = dot(keys, queries, 1, 1)
-    dots = dot(values, upstream, 1, 1)
+def prompt_head(at, q_ref, u_ref, qt_ref, ut_ref, start, keys, values, stats_ref):
+    scores = dot(keys, qt_ref[:, at], 1, 0)
+    dots = dot(values, ut_ref[:, at], 1, 0)
     own_highest = stats_ref[0:1, at]
     highest = jnp.maximum(own_highest, jnp.max(scores, axis=0, keepdims=True))
     own_factor = jnp.exp2((own_highest - highest) * LOG2_SCALE)
@@ -107,13 +115,13 @@
     factor = stats_ref[3:4, at] * inverse
     probs = weight * factor
     grads = probs * (dots - delta)
-    key_terms = dot(grads.astype(jnp.bfloat16), queries, 1, 0) * SCALING
-    value_terms = dot(probs.astype(jnp.bfloat16), upstream, 1, 0)
+    key_terms = dot(grads.astype(jnp.bfloat16), stacked(q_ref, start), 1, 0) * SCALING
+    value_terms = dot(probs.astype(jnp.bfloat16), stacked(u_ref, start), 1, 0)
     return key_terms, value_terms, own_factor * factor, delta
 
 
 def pair_kernel(
-    count, step, q_ref, u_ref, stats_ref, near_ref, far_ref,
+    count, step, q_ref, u_ref, qt_ref, ut_ref, stats_ref, near_ref, far_ref,
     scale_ref, near_terms_ref, far_terms_ref, kv_ref, terms_ref,
 ):
     seq = q_ref.shape[1]
@@ -125,11 +133,10 @@
     size = PER_HEAD * HEAD
     for i in range(heads):
         start = pl.multiple_of((pair * heads + i) * size, size)
-        queries, upstream = stacked(q_ref, start), stacked(u_ref, start)
         at = slice(i * HEAD, (i + 1) * HEAD)
         stats_at = pl.ds(pl.multiple_of((pair * heads + i) * PER_HEAD * seq, PER_HEAD * seq), PER_HEAD * seq)
         key_terms, value_terms, factor, delta = prompt_head(
-            stats_at, queries, upstream, kv_ref[0, :, at], kv_ref[1, :, at], stats_ref
+            stats_at, q_ref, u_ref, qt_ref, ut_ref, start, kv_ref[0, :, at], kv_ref[1, :, at], stats_ref
         )
         here = slice(i * PER_HEAD * seq, (i + 1) * PER_HEAD * seq)
         scale_ref[0:1, here] = factor
@@ -140,7 +147,7 @@
     far_terms_ref[...] = terms_ref[1 - side]
 
 
-def prompt_kernel(count, q_ref, u_ref, stats_ref, *refs):
+def prompt_kernel(count, q_ref, u_ref, qt_ref, ut_ref, stats_ref, *refs):
     blocks = refs[:count]
     scale_ref = refs[count]
     terms_refs = refs[count + 1 : 2 * count + 1]
@@ -171,7 +178,7 @@
         at = slice(j * PER_HEAD * seq, (j + 1) * PER_HEAD * seq)
         start = j * PER_HEAD * HEAD
         key_terms, value_terms, factor, delta = prompt_head(
-            at, stacked(q_ref, start), stacked(u_ref, start),
+            at, q_ref, u_ref, qt_ref, ut_ref, start,
             prompt_of(j * HEAD), prompt_of((KV_HEADS + j) * HEAD), stats_ref,
         )
         scale_ref[0:1, at] = factor
@@ -182,32 +189,56 @@
         terms_refs[step][...] = terms_ref[partner_of(me, step, count)].astype(jnp.bfloat16)
 
 
-def own_grad_kernel(steps, count, q_ref, u_ref, exp_ref, dots_ref, *refs):
+def first_head(step, count, heads):
+    if heads == KV_HEADS:
+        return 0
+    return lax.rem(lax.axis_index("resp") ^ step, count // 2) * heads
+
+
+def own_grad(step, count, q_ref, u_ref, exp_ref, dots_ref, scale_ref, out_ref):
     seq = q_ref.shape[1]
-    gk_ref, gv_ref = refs[len(steps) :]
-    for step, scale_ref in zip(steps, refs):
-        heads = scale_ref.shape[1] // (PER_HEAD * seq)
-        first = 0
-        if len(steps) > 1:
-            first = lax.rem(lax.axis_index("resp") ^ step, count // 2) * heads
-        for j in range(heads):
-            probs, grads = [], []
-            for h in range(PER_HEAD):
-                here = slice((j * PER_HEAD + h) * seq, (j * PER_HEAD + h + 1) * seq)
-                start = ((first + j) * PER_HEAD + h) * seq
-                at = pl.ds(start if len(steps) == 1 else pl.multiple_of(start, seq), seq)
-                prob = exp_ref[:, at] * scale_ref[0:1, here]
-                grad = prob * (dots_ref[:, at] - scale_ref[1:2, here])
-                probs.append(prob.astype(jnp.bfloat16))
-                grads.append(grad.astype(jnp.bfloat16))
-            start, column = (first + j) * PER_HEAD * HEAD, (first + j) * HEAD
-            if len(steps) > 1:
-                start, column = pl.multiple_of(start, HEAD), pl.multiple_of(column, HEAD)
-            cols = pl.ds(column, HEAD)
-            keys = dot(jnp.concatenate(grads, axis=1), stacked(q_ref, start), 1, 0) * SCALING
-            values = dot(jnp.concatenate(probs, axis=1), stacked(u_ref, start), 1, 0)
-            gk_ref[0, :, cols] = keys.astype(jnp.bfloat16)
-            gv_ref[0, :, cols] = values.astype(jnp.bfloat16)
+    heads = scale_ref.shape[1] // (PER_HEAD * seq)
+    first = first_head(step, count, heads)
+    size = PER_HEAD * HEAD
+    for j in range(heads):
+        probs, grads = [], []
+        for h in range(PER_HEAD):
+            here = slice((j * PER_HEAD + h) * seq, (j * PER_HEAD + h + 1) * seq)
+            at = pl.ds(pl.multiple_of(((first + j) * PER_HEAD + h) * seq, seq), seq)
+            prob = exp_ref[:, at] * scale_ref[0:1, here]
+            grad = prob * (dots_ref[:, at] - scale_ref[1:2, here])
+            probs.append(prob.astype(jnp.bfloat16))
+            grads.append(grad.astype(jnp.bfloat16))
+        start = pl.multiple_of((first + j) * size, size)
+        cols = slice(j * HEAD, (j + 1) * HEAD)
+        keys = dot(jnp.concatenate(grads, axis=1), stacked(q_ref, start), 1, 0) * SCALING
+        values = dot(jnp.concatenate(probs, axis=1), stacked(u_ref, start), 1, 0)
+        out_ref[0, :, cols] = keys.astype(jnp.bfloat16)
+        out_ref[1, :, cols] = values.astype(jnp.bfloat16)
+
+
+def own_grad_kernel(step, count, *refs):
+    own_grad(step, count, *refs)
+
+
+def last_own_grad_kernel(steps, count, q_ref, u_ref, exp_ref, dots_ref, scale_ref, *refs):
+    parts, (gk_ref, gv_ref, held_ref, sems) = refs[: len(steps) - 1], refs[len(steps) - 1 :]
+    copies = []
+
+    def store(i, ref):
+        heads = ref.shape[2] // HEAD
+        first = first_head(steps[i], count, heads) * HEAD
+        at = pl.ds(pl.multiple_of(first, HEAD), heads * HEAD)
+        for side, target in enumerate((gk_ref, gv_ref)):
+            copies.append(pltpu.make_async_copy(ref.at[side], target.at[0, :, at], sems.at[side, i]))
+            copies[-1].start()
+
+    for i, ref in enumerate(parts):
+        store(i, ref)
+    own_grad(steps[-1], count, q_ref, u_ref, exp_ref, dots_ref, scale_ref, held_ref)
+    store(len(steps) - 1, held_ref)
+    for copy in copies:
+        copy.wait()
 
 
 def sum_kernel(*refs):
@@ -218,19 +249,27 @@
 
 
 def weight_kernel(chips, *refs):
-    grads, columns, out_ref = refs[: 2 * chips], refs[2 * chips : 3 * chips], refs[3 * chips]
-    left = jnp.concatenate([ref[...] for ref in grads], axis=0)
+    grads, columns, (out_ref, held_ref, sems) = refs[: 2 * chips], refs[2 * chips : 3 * chips], refs[3 * chips :]
     right = jnp.concatenate([ref[side] for side in range(2) for ref in columns], axis=0)
-    out_ref[...] = dot(left, right, 0, 0)
-
-
-def call(kernel, outs, inputs, scratch=(), kinds={}, flops=0, limit=24):
+    copies = []
+    width = held_ref.shape[0] // sems.shape[0]
+    for i in range(sems.shape[0]):
+        rows = slice(i * width, (i + 1) * width)
+        left = jnp.concatenate([ref[:, rows] for ref in grads], axis=0)
+        held_ref[rows] = dot(left, right, 0, 0)
+        copies.append(pltpu.make_async_copy(held_ref.at[rows], out_ref.at[rows], sems.at[i]))
+        copies[-1].start()
+    for copy in copies:
+        copy.wait()
+
+
+def call(kernel, outs, inputs, scratch=(), kinds={}, out_kind=pltpu.VMEM, flops=0, limit=24):
     size = sum(x.size * x.dtype.itemsize for x in list(inputs) + list(outs))
     return pl.pallas_call(
         kernel,
         out_shape=tuple(outs),
         in_specs=[pl.BlockSpec(memory_space=kinds.get(i, pltpu.VMEM)) for i in range(len(inputs))],
-        out_specs=tuple(pl.BlockSpec(memory_space=pltpu.VMEM) for _ in outs),
+        out_specs=tuple(pl.BlockSpec(memory_space=out_kind) for _ in outs),
         scratch_shapes=list(scratch),
         cost_estimate=pl.CostEstimate(flops=flops, bytes_accessed=size, transcendentals=0),
         compiler_params=pltpu.CompilerParams(vmem_limit_bytes=limit << 20),
@@ -268,16 +307,18 @@
     (mask,) = call(mask_kernel, [shape((seq, seq), f32)], [], flops=MASK_FLOPS)
     hidden_blocks = [prompt_hidden] + [over_resp(prompt_hidden, s) for s in range(1, resps)]
     wide = shape((seq, HEADS * seq), f32)
-    exps, dots, stats = call(
+    turned = shape((HEAD, HEADS * seq), bf16)
+    queries_t, upstream_t, exps, dots, stats = call(
         own_kernel,
-        [wide, wide, shape((8, HEADS * seq), f32)],
+        [turned, turned, wide, wide, shape((8, HEADS * seq), f32)],
         [mask, queries, upstream, resp_keys, resp_values, signs, lengths],
         flops=OWN_FLOPS,
     )
+    (weight_t,) = call(turn_kernel, [shape((width, features), bf16)], [kv_weight])
     prompt_kv, hidden = call(
         functools.partial(project_kernel, resps),
         [block, shape((resps, rows, width), bf16)],
-        hidden_blocks + [kv_weight],
+        hidden_blocks + [weight_t],
         flops=2 * prompt * features * width,
     )
     kv_blocks = [prompt_kv] + [over_resp(prompt_kv, s) for s in range(1, resps)]
@@ -289,7 +330,7 @@
             scale, terms[s], terms[s + half] = call(
                 functools.partial(pair_kernel, resps, s),
                 [shape((8, features // HEAD * PER_HEAD * seq), f32), block, block],
-                [queries, upstream, stats, kv_blocks[s], kv_blocks[s + half]],
+                [queries, upstream, queries_t, upstream_t, stats, kv_blocks[s], kv_blocks[s + half]],
                 scratch=[pltpu.VMEM((2, prompt, features), bf16)] * 2,
                 flops=unit // half,
             )
@@ -299,7 +340,7 @@
         scale, *terms = call(
             functools.partial(prompt_kernel, resps),
             [shape((8, HEADS * seq), f32)] + [block] * resps,
-            [queries, upstream, stats] + kv_blocks,
+            [queries, upstream, queries_t, upstream_t, stats] + kv_blocks,
             scratch=[
                 pltpu.VMEM((resps, prompt, features), bf16),
                 pltpu.VMEM((resps, prompt, features), f32),
@@ -318,16 +359,35 @@
     (prompt_grad,) = call(sum_kernel, [block], terms)
     grad_columns = [prompt_grad] + [over_chips(prompt_grad, s) for s in range(1, chips)]
     grad_columns = grad_columns + [swap(x) for x in grad_columns]
+    halves = []
+    for step, scale in zip(steps[:-1], scales):
+        (own,) = call(
+            functools.partial(own_grad_kernel, step, resps),
+            [shape((2, seq, scale.shape[1] // (PER_HEAD * seq) * HEAD), bf16)],
+            [queries, upstream, exps, dots, scale],
+            flops=2 * unit // len(steps),
+        )
+        halves.append(own)
     grad_keys, grad_values = call(
-        functools.partial(own_grad_kernel, steps, resps),
+        functools.partial(last_own_grad_kernel, steps, resps),
         [shape(resp_keys.shape, bf16), shape(resp_values.shape, bf16)],
-        [queries, upstream, exps, dots] + scales,
-        flops=2 * unit,
+        [queries, upstream, exps, dots, scales[-1]] + halves,
+        scratch=[
+            pltpu.VMEM((2, seq, scales[-1].shape[1] // (PER_HEAD * seq) * HEAD), bf16),
+            pltpu.SemaphoreType.DMA((2, len(steps))),
+        ],
+        out_kind=pl.ANY,
+        flops=2 * unit // len(steps),
     )
     (grad_weight,) = call(
         functools.partial(weight_kernel, chips),
         [shape((features, columns), f32)],
         grad_columns + hidden_columns,
+        scratch=[
+            pltpu.VMEM((features, columns), f32),
+            pltpu.SemaphoreType.DMA((max(1, features // HEAD),)),
+        ],
+        out_kind=pl.ANY,
         flops=2 * groups * prompt * features * columns,
     )
     return (grad_keys, grad_values, grad_weight)

time: 44.3 us -> 43.2 us (0.975)
  waiting for transfers between devices: 12.3 us -> 11.1 us
    ppermute x9, waiting for transfers between devices: 9.05 us -> 7.99 us  [over_resp(): return lax.ppermute(value, 'resp', pairs)]
    pallas_call x9 -> x11, Pallas kernels: 8.87 us -> 9.07 us  [call(): pl.pallas_call(kernel, out_shape=tuple(outs), in_specs=[pl.BlockSpec(memo...]
  transfers between devices with their start and end apart: 20 -> 20, of which waited for: 7 -> 6; matrix products, arithmetic and copies ran while one was open for 0% -> 0% of each run, Pallas kernels for 14% -> 16%
where the time goes in v1:
time: 43.2 us; the launch traced here: 43.1 us
  starting transfers between devices  21.4 us (50%)
  waiting for transfers between devices  11.1 us (26%)
  Pallas kernels  9.07 us (21%)
  between operations  1.5 us (3%)
    ppermute x9, starting transfers between devices, over_resp(): return lax.ppermute(value, 'resp', pairs)  13.7 us
    pallas_call x11, Pallas kernels, call(): pl.pallas_call(kernel, out_shape=tuple(outs), in_specs=[pl.BlockSpec(memo...  9.07 us
    ppermute x9, waiting for transfers between devices, over_resp(): return lax.ppermute(value, 'resp', pairs)  7.99 us
    ppermute x6, starting transfers between devices, over_chips(): return lax.ppermute(value, 'group', pairs)  7.11 us
    ppermute x6, waiting for transfers between devices, over_chips(): return lax.ppermute(value, 'group', pairs)  3.12 us
  transfers between devices with their start and end apart: 20, of which 6 were waited for; matrix products, arithmetic and copies ran while one was open for 0% of the time, Pallas kernels for 16%

profile of v1, /device:TPU:0, one launch (start us, length us, event | category | flops | bytes accessed | tf_op | source)
XLA Modules:
  0.0 43.1 jit_solution(9488013091968223673)
XLA Ops:
  0.6 4.1 %collective-permute-start.1 = (bf16[1,8,4096]{2,1,0:T(8,128)(2,1)}, bf16[1,8,4096]{2,1,0:T(8,128)(2,1)S(1)}, u32[]{:S(2)}, u32[]{:S(2)}) collective-permute-start(bf16[1,8,4096]{2,1,0:T(8,128)(2,1)} %refs_0_.2), channel_id=1, source_target_pairs={{0,2},{1,3},{2,0},{3,1},{4,6},{5,7},{6,4},{7,5},{8,10},{9,11},{10,... | collective-permute-start | bytes 196616 | tf_op jit(solution)/shard_map/ppermute | solution.py:290
  4.8 1.6 %collective-permute-start = (bf16[1,8,4096]{2,1,0:T(8,128)(2,1)}, bf16[1,8,4096]{2,1,0:T(8,128)(2,1)S(1)}, u32[]{:S(2)}, u32[]{:S(2)}) collective-permute-start(bf16[1,8,4096]{2,1,0:T(8,128)(2,1)} %refs_0_.2), channel_id=1, source_target_pairs={{0,1},{1,0},{2,3},{3,2},{4,5},{5,4},{6,7},{7,6},{8,9},{9,8},{10,11... | collective-permute-start | bytes 196616 | tf_op jit(solution)/shard_map/ppermute | solution.py:290
  6.3 0.0 collective-permute-start.2
  7.0 0.0 copy-start.3
  7.0 1.1 %shard_map.105.refs_4_ = bf16[4096,512]{1,0:T(8,128)(2,1)S(1)} custom-call(bf16[512,4096]{1,0:T(8,128)(2,1)S(1)} %copy-done.2), custom_call_target="tpu_custom_call" | custom-call | bytes 8388608 | tf_op jit(solution)/shard_map/pallas_call | solution.py:268
  8.2 0.0 copy-start
  8.2 0.0 copy-start.1
  8.2 0.0 copy-start.4
  8.2 0.0 copy-start.5
  8.2 0.0 copy-start.6
  8.2 0.0 collective-permute-done.1.refs_2_
  8.2 1.0 %collective-permute-done.refs_1_ = bf16[1,8,4096]{2,1,0:T(8,128)(2,1)S(1)} collective-permute-done((bf16[1,8,4096]{2,1,0:T(8,128)(2,1)}, bf16[1,8,4096]{2,1,0:T(8,128)(2,1)S(1)}, u32[]{:S(2)}, u32[]{:S(2)}) %collective-permute-start) | collective-permute-done | bytes 65568 | tf_op jit(solution)/shard_map/ppermute | solution.py:290
  9.2 3.4 %collective-permute-done.2.refs_3_ = bf16[1,8,4096]{2,1,0:T(8,128)(2,1)S(1)} collective-permute-done((bf16[1,8,4096]{2,1,0:T(8,128)(2,1)}, bf16[1,8,4096]{2,1,0:T(8,128)(2,1)S(1)}, u32[]{:S(2)}, u32[]{:S(2)}) %collective-permute-start.2) | collective-permute-done | bytes 65568 | tf_op jit(solution)/shard_map/ppermute | solution.py:290
  12.6 0.8 %shard_map.106 = (bf16[32,512]{1,0:T(8,128)(2,1)S(1)}, bf16[4,8,4096]{2,1,0:T(8,128)(2,1)S(1)}) custom-call(bf16[1,8,4096]{2,1,0:T(8,128)(2,1)S(1)} %copy-done.3, bf16[1,8,4096]{2,1,0:T(8,128)(2,1)S(1)} %collective-permute-done.refs_1_, bf16[1,8,4096]{2,1,0:T(8,128)(2,1)S(1)} %collective-permute-done.1.refs_2_, ...), custom_call_target="tpu_custom_call" | custom-call | flops 134217728 | bytes 4751360 | tf_op jit(solution)/shard_map/pallas_call | solution.py:268
  13.4 1.3 %collective-permute-start.5 = (bf16[32,512]{1,0:T(8,128)(2,1)S(1)}, bf16[32,512]{1,0:T(8,128)(2,1)S(1)}, u32[]{:S(2)}, u32[]{:S(2)}) collective-permute-start(bf16[32,512]{1,0:T(8,128)(2,1)S(1)} %get-tuple-element.27.near_ref), channel_id=1, source_target_pairs={{0,2},{1,3},{2,0},{3,1},{4,6},{5,7},{6,4},{7,5},{8,10},{9,11},{10,... | collective-permute-start | bytes 98312 | tf_op jit(solution)/shard_map/ppermute | solution.py:290
  14.8 0.6 %collective-permute-start.4 = (bf16[32,512]{1,0:T(8,128)(2,1)S(1)}, bf16[32,512]{1,0:T(8,128)(2,1)S(1)}, u32[]{:S(2)}, u32[]{:S(2)}) collective-permute-start(bf16[32,512]{1,0:T(8,128)(2,1)S(1)} %get-tuple-element.27.near_ref), channel_id=1, source_target_pairs={{0,3},{1,2},{2,1},{3,0},{4,7},{5,6},{6,5},{7,4},{8,11},{9,10},{10,... | collective-permute-start | bytes 98312 | tf_op jit(solution)/shard_map/ppermute | solution.py:290
  15.3 1.6 %collective-permute-start.3 = (bf16[32,512]{1,0:T(8,128)(2,1)S(1)}, bf16[32,512]{1,0:T(8,128)(2,1)S(1)}, u32[]{:S(2)}, u32[]{:S(2)}) collective-permute-start(bf16[32,512]{1,0:T(8,128)(2,1)S(1)} %get-tuple-element.27.near_ref), channel_id=1, source_target_pairs={{0,1},{1,0},{2,3},{3,2},{4,5},{5,4},{6,7},{7,6},{8,9},{9,8},{10,11... | collective-permute-start | bytes 98312 | tf_op jit(solution)/shard_map/ppermute | solution.py:290
  17.0 1.3 %shard_map.104 = (bf16[128,4096]{1,0:T(8,128)(2,1)S(1)}, bf16[128,4096]{1,0:T(8,128)(2,1)S(1)}, f32[128,4096]{1,0:T(8,128)S(1)}, f32[128,4096]{1,0:T(8,128)S(1)}, f32[8,4096]{1,0:T(8,128)S(1)}) custom-call(f32[128,128]{1,0:T(8,128)S(1)} %shard_map.103.mask_ref, bf16[1,128,4096]{2,1,0:T(8,128)(2,1)S(1)} %copy-done, bf16[1,128,4096]{2,1,0:T(8,128)(2,1)S(1)} %copy-done.1, ...), custom_call_target="tpu_custom_call" | custom-call | flops 20000000000 | bytes 9110020 | tf_op jit(solution)/shard_map/pallas_call | solution.py:268
  18.3 0.0 collective-permute-done.5.far_ref
  18.3 1.1 %shard_map.108 = (f32[8,2048]{1,0:T(8,128)S(1)}, bf16[32,512]{1,0:T(8,128)(2,1)S(1)}, bf16[32,512]{1,0:T(8,128)(2,1)S(1)}) custom-call(bf16[1,128,4096]{2,1,0:T(8,128)(2,1)S(1)} %copy-done, bf16[1,128,4096]{2,1,0:T(8,128)(2,1)S(1)} %copy-done.1, bf16[128,4096]{1,0:T(8,128)(2,1)S(1)} %get-tuple-element.24.qt_ref, ...), custom_call_target="tpu_custom_call" | custom-call | flops 67108864 | bytes 4521984 | tf_op jit(solution)/shard_map/pallas_call | solution.py:268
  19.4 2.3 %collective-permute-start.7 = (bf16[32,512]{1,0:T(8,128)(2,1)S(1)}, bf16[32,512]{1,0:T(8,128)(2,1)S(1)}, u32[]{:S(2)}, u32[]{:S(2)}) collective-permute-start(bf16[32,512]{1,0:T(8,128)(2,1)S(1)} %get-tuple-element.34), channel_id=1, source_target_pairs={{0,2},{1,3},{2,0},{3,1},{4,6},{5,7},{6,4},{7,5},{8,10},{9,11},{10,... | collective-permute-start | bytes 98312 | tf_op jit(solution)/shard_map/ppermute | solution.py:290
  21.7 0.0 collective-permute-done.4.far_ref
  21.7 1.1 %shard_map.107 = (f32[8,2048]{1,0:T(8,128)S(1)}, bf16[32,512]{1,0:T(8,128)(2,1)S(1)}, bf16[32,512]{1,0:T(8,128)(2,1)S(1)}) custom-call(bf16[1,128,4096]{2,1,0:T(8,128)(2,1)S(1)} %copy-done, bf16[1,128,4096]{2,1,0:T(8,128)(2,1)S(1)} %copy-done.1, bf16[128,4096]{1,0:T(8,128)(2,1)S(1)} %get-tuple-element.24.qt_ref, ...), custom_call_target="tpu_custom_call" | custom-call | flops 67108864 | bytes 4521984 | tf_op jit(solution)/shard_map/pallas_call | solution.py:268
  22.8 0.1 collective-permute-start.6
  22.9 2.2 %collective-permute-start.8 = (bf16[32,512]{1,0:T(8,128)(2,1)S(1)}, bf16[32,512]{1,0:T(8,128)(2,1)S(1)}, u32[]{:S(2)}, u32[]{:S(2)}) collective-permute-start(bf16[32,512]{1,0:T(8,128)(2,1)S(1)} %get-tuple-element.35), channel_id=1, source_target_pairs={{0,3},{1,2},{2,1},{3,0},{4,7},{5,6},{6,5},{7,4},{8,11},{9,10},{10,... | collective-permute-start | bytes 98312 | tf_op jit(solution)/shard_map/ppermute | solution.py:290
  25.0 1.7 %collective-permute-done.6.refs_1_ = bf16[32,512]{1,0:T(8,128)(2,1)S(1)} collective-permute-done((bf16[32,512]{1,0:T(8,128)(2,1)S(1)}, bf16[32,512]{1,0:T(8,128)(2,1)S(1)}, u32[]{:S(2)}, u32[]{:S(2)}) %collective-permute-start.6) | collective-permute-done | bytes 32800 | tf_op jit(solution)/shard_map/ppermute | solution.py:290
  26.8 1.9 %collective-permute-done.8.refs_3_ = bf16[32,512]{1,0:T(8,128)(2,1)S(1)} collective-permute-done((bf16[32,512]{1,0:T(8,128)(2,1)S(1)}, bf16[32,512]{1,0:T(8,128)(2,1)S(1)}, u32[]{:S(2)}, u32[]{:S(2)}) %collective-permute-start.8) | collective-permute-done | bytes 32800 | tf_op jit(solution)/shard_map/ppermute | solution.py:290
  28.7 2.5 %collective-permute-start.11 = (bf16[32,512]{1,0:T(8,128)(2,1)S(1)}, bf16[32,512]{1,0:T(8,128)(2,1)S(1)}, u32[]{:S(2)}, u32[]{:S(2)}) collective-permute-start(bf16[32,512]{1,0:T(8,128)(2,1)S(1)} %shard_map.111.refs_0_), channel_id=1, source_target_pairs={{0,24},{4,28},{8,16},{12,20},{16,8},{20,12},{24,0},{28,4},{1,25},{... | collective-permute-start | bytes 98312 | tf_op jit(solution)/shard_map/ppermute | solution.py:294
  31.2 0.5 %collective-permute-start.10 = (bf16[32,512]{1,0:T(8,128)(2,1)S(1)}, bf16[32,512]{1,0:T(8,128)(2,1)S(1)}, u32[]{:S(2)}, u32[]{:S(2)}) collective-permute-start(bf16[32,512]{1,0:T(8,128)(2,1)S(1)} %shard_map.111.refs_0_), channel_id=1, source_target_pairs={{0,16},{4,20},{8,24},{12,28},{16,0},{20,4},{24,8},{28,12},{1,17},{... | collective-permute-start | bytes 98312 | tf_op jit(solution)/shard_map/ppermute | solution.py:294
  31.7 0.5 %collective-permute-start.9 = (bf16[32,512]{1,0:T(8,128)(2,1)S(1)}, bf16[32,512]{1,0:T(8,128)(2,1)S(1)}, u32[]{:S(2)}, u32[]{:S(2)}) collective-permute-start(bf16[32,512]{1,0:T(8,128)(2,1)S(1)} %shard_map.111.refs_0_), channel_id=1, source_target_pairs={{0,8},{4,12},{8,0},{12,4},{16,24},{20,28},{24,16},{28,20},{1,9},{5... | collective-permute-start | bytes 98312 | tf_op jit(solution)/shard_map/ppermute | solution.py:294
  32.2 1.3 %collective-permute-done.11.refs_3_ = bf16[32,512]{1,0:T(8,128)(2,1)S(1)} collective-permute-done((bf16[32,512]{1,0:T(8,128)(2,1)S(1)}, bf16[32,512]{1,0:T(8,128)(2,1)S(1)}, u32[]{:S(2)}, u32[]{:S(2)}) %collective-permute-start.11) | collective-permute-done | bytes 32800 | tf_op jit(solution)/shard_map/ppermute | solution.py:294
  33.6 0.0 collective-permute-start.15
  33.6 0.0 collective-permute-done.16.partner_ref
  33.6 1.6 %collective-permute-start.17 = (bf16[2,32,512]{2,1,0:T(8,128)(2,1)S(1)}, bf16[2,32,512]{2,1,0:T(8,128)(2,1)S(1)}, u32[]{:S(2)}, u32[]{:S(2)}) collective-permute-start(bf16[2,32,512]{2,1,0:T(8,128)(2,1)S(1)} %get-tuple-element.38), channel_id=1, source_target_pairs={{0,8},{4,12},{8,0},{12,4},{16,24},{20,28},{24,16},{28,20},{1,9},{5... | collective-permute-start | bytes 196616 | tf_op jit(solution)/shard_map/ppermute | solution.py:294
  35.2 1.5 %collective-permute-start.18 = (bf16[2,32,512]{2,1,0:T(8,128)(2,1)S(1)}, bf16[2,32,512]{2,1,0:T(8,128)(2,1)S(1)}, u32[]{:S(2)}, u32[]{:S(2)}) collective-permute-start(bf16[2,32,512]{2,1,0:T(8,128)(2,1)S(1)} %get-tuple-element.39), channel_id=1, source_target_pairs={{0,16},{4,20},{8,24},{12,28},{16,0},{20,4},{24,8},{28,12},{1,17},{... | collective-permute-start | bytes 196616 | tf_op jit(solution)/shard_map/ppermute | solution.py:294
  36.7 0.0 collective-permute-done.10.refs_2_
  36.7 0.4 %collective-permute-start.19 = (bf16[2,32,512]{2,1,0:T(8,128)(2,1)S(1)}, bf16[2,32,512]{2,1,0:T(8,128)(2,1)S(1)}, u32[]{:S(2)}, u32[]{:S(2)}) collective-permute-start(bf16[2,32,512]{2,1,0:T(8,128)(2,1)S(1)} %get-tuple-element.40), channel_id=1, source_target_pairs={{0,24},{4,28},{8,16},{12,20},{16,8},{20,12},{24,0},{28,4},{1,25},{... | collective-permute-start | bytes 196616 | tf_op jit(solution)/shard_map/ppermute | solution.py:294
  37.1 0.0 collective-permute-done.9.refs_1_
  37.1 0.0 collective-permute-start.14
  37.1 0.0 collective-permute-done.15.refs_7_
  37.2 0.5 %collective-permute-start.13 = (bf16[32,512]{1,0:T(8,128)(2,1)S(1)}, bf16[32,512]{1,0:T(8,128)(2,1)S(1)}, u32[]{:S(2)}, u32[]{:S(2)}) collective-permute-start(bf16[32,512]{1,0:T(8,128)(2,1)S(1)} %collective-permute-done.9.refs_1_), channel_id=1, source_target_pairs={{0,4},{4,0},{8,12},{12,8},{16,20},{20,16},{24,28},{28,24},{1,5},{5... | collective-permute-start | bytes 98312 | tf_op jit(solution)/shard_map/ppermute | solution.py:297
  37.7 0.8 %shard_map.109.refs_0_ = bf16[2,128,512]{2,1,0:T(8,128)(2,1)S(1)} custom-call(bf16[1,128,4096]{2,1,0:T(8,128)(2,1)S(1)} %copy-done, bf16[1,128,4096]{2,1,0:T(8,128)(2,1)S(1)} %copy-done.1, f32[128,4096]{1,0:T(8,128)S(1)} %get-tuple-element.22.refs_2_.exp_ref, f32[128,4096]{1,0:T(8,128)S(1)} %get-tuple-element.23.refs_3_.dots_ref, ...), custom_call_target="tpu_custom_call" | custom-call | flops 134217728 | bytes 6619136 | tf_op jit(solution)/shard_map/pallas_call | solution.py:268
  38.5 1.6 %shard_map.110 = (bf16[1,128,1024]{2,1,0:T(8,128)(2,1)}, bf16[1,128,1024]{2,1,0:T(8,128)(2,1)}) custom-call(bf16[1,128,4096]{2,1,0:T(8,128)(2,1)S(1)} %copy-done, bf16[1,128,4096]{2,1,0:T(8,128)(2,1)S(1)} %copy-done.1, f32[128,4096]{1,0:T(8,128)S(1)} %get-tuple-element.22.refs_2_.exp_ref, f32[128,4096]{1,0:T(8,128)S(1)} %get-tuple-element.23.refs_3_.dots_ref, ...), custom_call_target="tpu_custom_call" | custom-call | flops 134217728 | bytes 7143424 | tf_op jit(solution)/shard_map/pallas_call | solution.py:268
  40.0 0.0 collective-permute-done.14.refs_6_
  40.1 0.0 collective-permute-done.17.refs_9_
  40.1 0.0 collective-permute-done.18.refs_10_
  40.1 1.8 %collective-permute-done.19.refs_11_ = bf16[2,32,512]{2,1,0:T(8,128)(2,1)S(1)} collective-permute-done((bf16[2,32,512]{2,1,0:T(8,128)(2,1)S(1)}, bf16[2,32,512]{2,1,0:T(8,128)(2,1)S(1)}, u32[]{:S(2)}, u32[]{:S(2)}) %collective-permute-start.19) | collective-permute-done | bytes 65568 | tf_op jit(solution)/shard_map/ppermute | solution.py:294
  41.9 1.2 %shard_map.113 = f32[512,512]{1,0:T(8,128)} custom-call(bf16[32,512]{1,0:T(8,128)(2,1)S(1)} %shard_map.111.refs_0_, bf16[32,512]{1,0:T(8,128)(2,1)S(1)} %collective-permute-done.9.refs_1_, bf16[32,512]{1,0:T(8,128)(2,1)S(1)} %collective-permute-done.10.refs_2_, bf16[32,512]{1,0:T(8,128)(2,1)S(1)} %collective-permute-done.11.refs_3_, ...), custom_call_target="tpu_custom_call" | custom-call | flops 134217728 | bytes 1572864 | tf_op jit(solution)/shard_map/pallas_call | solution.py:268
  (17 shorter events, 0.1 us)
Async XLA Ops:
  0.6 6.4 %copy-start.2 = (bf16[512,4096]{1,0:T(8,128)(2,1)S(1)}, bf16[512,4096]{1,0:T(8,128)(2,1)}, u32[]{:S(2)}) copy-start(bf16[512,4096]{1,0:T(8,128)(2,1)} %w_ref.1) | copy-start | bytes 12582916
  0.6 7.6 %collective-permute-start.1 = (bf16[1,8,4096]{2,1,0:T(8,128)(2,1)}, bf16[1,8,4096]{2,1,0:T(8,128)(2,1)S(1)}, u32[]{:S(2)}, u32[]{:S(2)}) collective-permute-start(bf16[1,8,4096]{2,1,0:T(8,128)(2,1)} %refs_0_.2), channel_id=1, source_target_pairs={{0,2},{1,3},{2,0},{3,1},{4,6},{5,7},{6,4},{7,5},{8,10},{9,11},{10,... | collective-permute-start | bytes 196616 | tf_op jit(solution)/shard_map/ppermute | solution.py:290
  4.8 4.5 %collective-permute-start = (bf16[1,8,4096]{2,1,0:T(8,128)(2,1)}, bf16[1,8,4096]{2,1,0:T(8,128)(2,1)S(1)}, u32[]{:S(2)}, u32[]{:S(2)}) collective-permute-start(bf16[1,8,4096]{2,1,0:T(8,128)(2,1)} %refs_0_.2), channel_id=1, source_target_pairs={{0,1},{1,0},{2,3},{3,2},{4,5},{5,4},{6,7},{7,6},{8,9},{9,8},{10,11... | collective-permute-start | bytes 196616 | tf_op jit(solution)/shard_map/ppermute | solution.py:290
  6.3 6.3 %collective-permute-start.2 = (bf16[1,8,4096]{2,1,0:T(8,128)(2,1)}, bf16[1,8,4096]{2,1,0:T(8,128)(2,1)S(1)}, u32[]{:S(2)}, u32[]{:S(2)}) collective-permute-start(bf16[1,8,4096]{2,1,0:T(8,128)(2,1)} %refs_0_.2), channel_id=1, source_target_pairs={{0,3},{1,2},{2,1},{3,0},{4,7},{5,6},{6,5},{7,4},{8,11},{9,10},{10,... | collective-permute-start | bytes 196616 | tf_op jit(solution)/shard_map/ppermute | solution.py:290
  7.0 5.6 %copy-start.3 = (bf16[1,8,4096]{2,1,0:T(8,128)(2,1)S(1)}, bf16[1,8,4096]{2,1,0:T(8,128)(2,1)}, u32[]{:S(2)}) copy-start(bf16[1,8,4096]{2,1,0:T(8,128)(2,1)} %refs_0_.2) | copy-start | bytes 196612
  8.2 8.8 %copy-start = (bf16[1,128,4096]{2,1,0:T(8,128)(2,1)S(1)}, bf16[1,128,4096]{2,1,0:T(8,128)(2,1)}, u32[]{:S(2)}) copy-start(bf16[1,128,4096]{2,1,0:T(8,128)(2,1)} %q_ref.7) | copy-start | bytes 3145732
  8.2 8.8 %copy-start.1 = (bf16[1,128,4096]{2,1,0:T(8,128)(2,1)S(1)}, bf16[1,128,4096]{2,1,0:T(8,128)(2,1)}, u32[]{:S(2)}) copy-start(bf16[1,128,4096]{2,1,0:T(8,128)(2,1)} %u_ref.7) | copy-start | bytes 3145732
  8.2 8.8 %copy-start.4 = (bf16[1,128,1024]{2,1,0:T(8,128)(2,1)S(1)}, bf16[1,128,1024]{2,1,0:T(8,128)(2,1)}, u32[]{:S(2)}) copy-start(bf16[1,128,1024]{2,1,0:T(8,128)(2,1)} %k_ref.1) | copy-start | bytes 786436
  8.2 8.8 %copy-start.5 = (bf16[1,128,1024]{2,1,0:T(8,128)(2,1)S(1)}, bf16[1,128,1024]{2,1,0:T(8,128)(2,1)}, u32[]{:S(2)}) copy-start(bf16[1,128,1024]{2,1,0:T(8,128)(2,1)} %v_ref.1) | copy-start | bytes 786436
  8.2 8.8 %copy-start.6 = (s32[1,128]{1,0:T(1,128)S(1)}, s32[1,128]{1,0:T(1,128)}, u32[]{:S(2)}) copy-start(s32[1,128]{1,0:T(1,128)} %signs_ref.1) | copy-start | bytes 1540
  13.4 4.9 %collective-permute-start.5 = (bf16[32,512]{1,0:T(8,128)(2,1)S(1)}, bf16[32,512]{1,0:T(8,128)(2,1)S(1)}, u32[]{:S(2)}, u32[]{:S(2)}) collective-permute-start(bf16[32,512]{1,0:T(8,128)(2,1)S(1)} %get-tuple-element.27.near_ref), channel_id=1, source_target_pairs={{0,2},{1,3},{2,0},{3,1},{4,6},{5,7},{6,4},{7,5},{8,10},{9,11},{10,... | collective-permute-start | bytes 98312 | tf_op jit(solution)/shard_map/ppermute | solution.py:290
  14.8 6.9 %collective-permute-start.4 = (bf16[32,512]{1,0:T(8,128)(2,1)S(1)}, bf16[32,512]{1,0:T(8,128)(2,1)S(1)}, u32[]{:S(2)}, u32[]{:S(2)}) collective-permute-start(bf16[32,512]{1,0:T(8,128)(2,1)S(1)} %get-tuple-element.27.near_ref), channel_id=1, source_target_pairs={{0,3},{1,2},{2,1},{3,0},{4,7},{5,6},{6,5},{7,4},{8,11},{9,10},{10,... | collective-permute-start | bytes 98312 | tf_op jit(solution)/shard_map/ppermute | solution.py:290
  15.3 6.4 %collective-permute-start.3 = (bf16[32,512]{1,0:T(8,128)(2,1)S(1)}, bf16[32,512]{1,0:T(8,128)(2,1)S(1)}, u32[]{:S(2)}, u32[]{:S(2)}) collective-permute-start(bf16[32,512]{1,0:T(8,128)(2,1)S(1)} %get-tuple-element.27.near_ref), channel_id=1, source_target_pairs={{0,1},{1,0},{2,3},{3,2},{4,5},{5,4},{6,7},{7,6},{8,9},{9,8},{10,11... | collective-permute-start | bytes 98312 | tf_op jit(solution)/shard_map/ppermute | solution.py:290
  16.9 16.6 %collective-permute-start.16 = (bf16[4,8,4096]{2,1,0:T(8,128)(2,1)S(1)}, bf16[4,8,4096]{2,1,0:T(8,128)(2,1)S(1)}, u32[]{:S(2)}, u32[]{:S(2)}) collective-permute-start(bf16[4,8,4096]{2,1,0:T(8,128)(2,1)S(1)} %get-tuple-element.36.mine_ref), channel_id=1, source_target_pairs={{0,4},{4,0},{8,12},{12,8},{16,20},{20,16},{24,28},{28,24},{1,5},{5... | collective-permute-start | bytes 786440 | tf_op jit(solution)/shard_map/ppermute | solution.py:297
  19.4 5.6 %collective-permute-start.7 = (bf16[32,512]{1,0:T(8,128)(2,1)S(1)}, bf16[32,512]{1,0:T(8,128)(2,1)S(1)}, u32[]{:S(2)}, u32[]{:S(2)}) collective-permute-start(bf16[32,512]{1,0:T(8,128)(2,1)S(1)} %get-tuple-element.34), channel_id=1, source_target_pairs={{0,2},{1,3},{2,0},{3,1},{4,6},{5,7},{6,4},{7,5},{8,10},{9,11},{10,... | collective-permute-start | bytes 98312 | tf_op jit(solution)/shard_map/ppermute | solution.py:290
  22.8 4.0 %collective-permute-start.6 = (bf16[32,512]{1,0:T(8,128)(2,1)S(1)}, bf16[32,512]{1,0:T(8,128)(2,1)S(1)}, u32[]{:S(2)}, u32[]{:S(2)}) collective-permute-start(bf16[32,512]{1,0:T(8,128)(2,1)S(1)} %get-tuple-element.33), channel_id=1, source_target_pairs={{0,1},{1,0},{2,3},{3,2},{4,5},{5,4},{6,7},{7,6},{8,9},{9,8},{10,11... | collective-permute-start | bytes 98312 | tf_op jit(solution)/shard_map/ppermute | solution.py:290
  22.9 5.8 %collective-permute-start.8 = (bf16[32,512]{1,0:T(8,128)(2,1)S(1)}, bf16[32,512]{1,0:T(8,128)(2,1)S(1)}, u32[]{:S(2)}, u32[]{:S(2)}) collective-permute-start(bf16[32,512]{1,0:T(8,128)(2,1)S(1)} %get-tuple-element.35), channel_id=1, source_target_pairs={{0,3},{1,2},{2,1},{3,0},{4,7},{5,6},{6,5},{7,4},{8,11},{9,10},{10,... | collective-permute-start | bytes 98312 | tf_op jit(solution)/shard_map/ppermute | solution.py:290
  28.7 4.9 %collective-permute-start.11 = (bf16[32,512]{1,0:T(8,128)(2,1)S(1)}, bf16[32,512]{1,0:T(8,128)(2,1)S(1)}, u32[]{:S(2)}, u32[]{:S(2)}) collective-permute-start(bf16[32,512]{1,0:T(8,128)(2,1)S(1)} %shard_map.111.refs_0_), channel_id=1, source_target_pairs={{0,24},{4,28},{8,16},{12,20},{16,8},{20,12},{24,0},{28,4},{1,25},{... | collective-permute-start | bytes 98312 | tf_op jit(solution)/shard_map/ppermute | solution.py:294
  31.2 4.0 %collective-permute-start.12 = (bf16[32,512]{1,0:T(8,128)(2,1)S(1)}, bf16[32,512]{1,0:T(8,128)(2,1)S(1)}, u32[]{:S(2)}, u32[]{:S(2)}) collective-permute-start(bf16[32,512]{1,0:T(8,128)(2,1)S(1)} %shard_map.111.refs_0_), channel_id=1, source_target_pairs={{0,4},{4,0},{8,12},{12,8},{16,20},{20,16},{24,28},{28,24},{1,5},{5... | collective-permute-start | bytes 98312 | tf_op jit(solution)/shard_map/ppermute | solution.py:297
  31.2 5.5 %collective-permute-start.10 = (bf16[32,512]{1,0:T(8,128)(2,1)S(1)}, bf16[32,512]{1,0:T(8,128)(2,1)S(1)}, u32[]{:S(2)}, u32[]{:S(2)}) collective-permute-start(bf16[32,512]{1,0:T(8,128)(2,1)S(1)} %shard_map.111.refs_0_), channel_id=1, source_target_pairs={{0,16},{4,20},{8,24},{12,28},{16,0},{20,4},{24,8},{28,12},{1,17},{... | collective-permute-start | bytes 98312 | tf_op jit(solution)/shard_map/ppermute | solution.py:294
  31.7 5.5 %collective-permute-start.9 = (bf16[32,512]{1,0:T(8,128)(2,1)S(1)}, bf16[32,512]{1,0:T(8,128)(2,1)S(1)}, u32[]{:S(2)}, u32[]{:S(2)}) collective-permute-start(bf16[32,512]{1,0:T(8,128)(2,1)S(1)} %shard_map.111.refs_0_), channel_id=1, source_target_pairs={{0,8},{4,12},{8,0},{12,4},{16,24},{20,28},{24,16},{28,20},{1,9},{5... | collective-permute-start | bytes 98312 | tf_op jit(solution)/shard_map/ppermute | solution.py:294
  33.6 3.6 %collective-permute-start.15 = (bf16[32,512]{1,0:T(8,128)(2,1)S(1)}, bf16[32,512]{1,0:T(8,128)(2,1)S(1)}, u32[]{:S(2)}, u32[]{:S(2)}) collective-permute-start(bf16[32,512]{1,0:T(8,128)(2,1)S(1)} %collective-permute-done.11.refs_3_), channel_id=1, source_target_pairs={{0,4},{4,0},{8,12},{12,8},{16,20},{20,16},{24,28},{28,24},{1,5},{5... | collective-permute-start | bytes 98312 | tf_op jit(solution)/shard_map/ppermute | solution.py:297
  33.6 6.5 %collective-permute-start.17 = (bf16[2,32,512]{2,1,0:T(8,128)(2,1)S(1)}, bf16[2,32,512]{2,1,0:T(8,128)(2,1)S(1)}, u32[]{:S(2)}, u32[]{:S(2)}) collective-permute-start(bf16[2,32,512]{2,1,0:T(8,128)(2,1)S(1)} %get-tuple-element.38), channel_id=1, source_target_pairs={{0,8},{4,12},{8,0},{12,4},{16,24},{20,28},{24,16},{28,20},{1,9},{5... | collective-permute-start | bytes 196616 | tf_op jit(solution)/shard_map/ppermute | solution.py:294
  35.2 4.9 %collective-permute-start.18 = (bf16[2,32,512]{2,1,0:T(8,128)(2,1)S(1)}, bf16[2,32,512]{2,1,0:T(8,128)(2,1)S(1)}, u32[]{:S(2)}, u32[]{:S(2)}) collective-permute-start(bf16[2,32,512]{2,1,0:T(8,128)(2,1)S(1)} %get-tuple-element.39), channel_id=1, source_target_pairs={{0,16},{4,20},{8,24},{12,28},{16,0},{20,4},{24,8},{28,12},{1,17},{... | collective-permute-start | bytes 196616 | tf_op jit(solution)/shard_map/ppermute | solution.py:294
  36.7 5.2 %collective-permute-start.19 = (bf16[2,32,512]{2,1,0:T(8,128)(2,1)S(1)}, bf16[2,32,512]{2,1,0:T(8,128)(2,1)S(1)}, u32[]{:S(2)}, u32[]{:S(2)}) collective-permute-start(bf16[2,32,512]{2,1,0:T(8,128)(2,1)S(1)} %get-tuple-element.40), channel_id=1, source_target_pairs={{0,24},{4,28},{8,16},{12,20},{16,8},{20,12},{24,0},{28,4},{1,25},{... | collective-permute-start | bytes 196616 | tf_op jit(solution)/shard_map/ppermute | solution.py:294
  37.1 2.9 %collective-permute-start.14 = (bf16[32,512]{1,0:T(8,128)(2,1)S(1)}, bf16[32,512]{1,0:T(8,128)(2,1)S(1)}, u32[]{:S(2)}, u32[]{:S(2)}) collective-permute-start(bf16[32,512]{1,0:T(8,128)(2,1)S(1)} %collective-permute-done.10.refs_2_), channel_id=1, source_target_pairs={{0,4},{4,0},{8,12},{12,8},{16,20},{20,16},{24,28},{28,24},{1,5},{5... | collective-permute-start | bytes 98312 | tf_op jit(solution)/shard_map/ppermute | solution.py:297
  37.2 2.9 %collective-permute-start.13 = (bf16[32,512]{1,0:T(8,128)(2,1)S(1)}, bf16[32,512]{1,0:T(8,128)(2,1)S(1)}, u32[]{:S(2)}, u32[]{:S(2)}) collective-permute-start(bf16[32,512]{1,0:T(8,128)(2,1)S(1)} %collective-permute-done.9.refs_1_), channel_id=1, source_target_pairs={{0,4},{4,0},{8,12},{12,8},{16,20},{20,16},{24,28},{28,24},{1,5},{5... | collective-permute-start | bytes 98312 | tf_op jit(solution)/shard_map/ppermute | solution.py:297
